TPU v7x, 512 devices: a whole 4x4x16 slice. The times are simulated.
512 devices in a mesh: gx: 16 (over z), gy: 8 (over y, x_lo), gz: 4 (over x_hi, core).
Axes of the slice: x: 4 (x_hi: 2, x_lo: 2; x = x_hi * 2 + x_lo), y: 4, z: 16, core: 2. Of those that a mesh axis runs over, the one named last changes fastest.
Arguments:
- start_disp: float32 [3, 128, 64, 512], P(None, 'gx', 'gy', 'gz'), may hold values from -2 to 2
- inertial: float32 [3, 128, 64, 512], P(None, 'gx', 'gy', 'gz'), may hold values from -1 to 1
- material: int32 [128, 64, 512], P('gx', 'gy', 'gz'), may hold values from 0 to 7
- pinned: int32 [128, 64, 512], P('gx', 'gy', 'gz'), may hold values 0 or 1
- stiffness: float32 [8], replicated, may hold values from 3 to 100
Outputs:
- displacement: float32 [3, 128, 64, 512], P(None, 'gx', 'gy', 'gz')
All inputs are finite; a program needn't handle non-finite values. No bound on the sum of `pinned` on one device may be relied on, other than what follows from the above.
Results may differ from a plain program's by a relative error of at most 0.0003.
Values sent between devices are 32-bit elements; how exact they have to be, the bound alone decides.
A program may use at most 64 MiB of HBM per device.

v0:
```python
import jax
import jax.numpy as jnp
from jax import lax
from jax.sharding import PartitionSpec as P

ITERS = 4
POLAR_STEPS = 6
MATS = 8


inertia = 1.0
relax = 0.6
radius = 0.9


def with_halo(cells, sides, width):
    for axis, dim in sides:
        count = lax.axis_size(axis)
        ends = count - 1
        head = lax.slice_in_dim(cells, 0, width, axis=dim)
        tail = lax.slice_in_dim(cells, cells.shape[dim] - width, cells.shape[dim], axis=dim)
        cells = jnp.concatenate(
            [
                lax.ppermute(tail, axis, [(i, (i + 1) % count) for i in range(ends)]),
                cells,
                lax.ppermute(head, axis, [((i + 1) % count, i) for i in range(ends)]),
            ],
            axis=dim,
        )
    return cells


def forward_diff(field, axis):
    size = field.shape[axis]
    return lax.slice_in_dim(field, 1, size, axis=axis) - lax.slice_in_dim(
        field, 0, size - 1, axis=axis
    )


def pair_sum(field, axis):
    size = field.shape[axis]
    return lax.slice_in_dim(field, 1, size, axis=axis) + lax.slice_in_dim(
        field, 0, size - 1, axis=axis
    )


def gradient(field, axis):
    result = forward_diff(field, axis)
    for other in range(3):
        if other != axis:
            result = pair_sum(result, other)
    return 0.25 * result


def project(nodes, welem):
    deform = [
        [gradient(nodes[c], d) + (1.0 if c == d else 0.0) for d in range(3)] for c in range(3)
    ]
    total = sum((deform[c][d] * deform[c][d] for c in range(3) for d in range(3)))
    scale = jnp.maximum(jnp.sqrt(total / 3.0), 1.0)
    rotate = [[deform[c][d] / scale for d in range(3)] for c in range(3)]
    for step in range(POLAR_STEPS):
        middle = [
            [
                (1.5 if i == j else 0.0)
                - 0.5 * sum((rotate[k][i] * rotate[k][j] for k in range(3)))
                for j in range(3)
            ]
            for i in range(3)
        ]
        rotate = [
            [sum((rotate[c][j] * middle[j][d] for j in range(3))) for d in range(3)]
            for c in range(3)
        ]
    return [welem * (deform[c][d] - rotate[c][d]) for c in range(3) for d in range(3)]


def assemble(stress):
    forces = []
    for c in range(3):
        total = 0.0
        for d in range(3):
            term = stress[3 * c + d]
            for other in range(3):
                if other != d:
                    term = pair_sum(term, other)
            total = total - 0.25 * forward_diff(term, d)
        forces.append(total)
    return jnp.stack(forces)


def diagonal(welem):
    total = welem
    for axis in range(3):
        total = pair_sum(total, axis)
    return inertia + 3.0 / 16.0 * total


def node_halo(disp, weights):
    joined = jnp.concatenate([disp, weights[None]], axis=0)
    return with_halo(joined, (("gx", 1), ("gy", 2), ("gz", 3)), 1)


def per_device(start_disp, inertial, material, pinned, stiffness):
    size_x, size_y, size_z = material.shape
    grid_x = lax.broadcasted_iota(jnp.int32, material.shape, 0) + lax.axis_index("gx") * size_x
    grid_y = lax.broadcasted_iota(jnp.int32, material.shape, 1) + lax.axis_index("gy") * size_y
    grid_z = lax.broadcasted_iota(jnp.int32, material.shape, 2) + lax.axis_index("gz") * size_z
    valid = (
        (grid_x < size_x * lax.axis_size("gx") - 1)
        & (grid_y < size_y * lax.axis_size("gy") - 1)
        & (grid_z < size_z * lax.axis_size("gz") - 1)
    )
    table = jnp.zeros(material.shape, jnp.float32)
    for index in range(MATS):
        table = table + jnp.where(material == index, stiffness[index], 0.0)
    weights = jnp.where(valid, table, 0.0)
    pins = pinned[None] > 0
    disp = jnp.where(pins, inertial, start_disp)
    previous = disp
    omega = 1.0
    for step in range(ITERS):
        padded = node_halo(disp, weights)
        welem = padded[3, : size_x + 1, : size_y + 1, : size_z + 1]
        diag = diagonal(welem)
        forces = assemble(project([padded[0], padded[1], padded[2]], welem))
        target = disp - relax * (inertia * (disp - inertial) + forces) / diag[None]
        if step == 0:
            fresh = target
        else:
            omega = (
                2.0 / (2.0 - radius * radius)
                if step == 1
                else 4.0 / (4.0 - radius * radius * omega)
            )
            fresh = omega * (target - previous) + previous
        fresh = jnp.where(pins, inertial, fresh)
        previous = disp
        disp = fresh
    return disp


def solution(mesh):
    placed = (
        P(None, "gx", "gy", "gz"),
        P(None, "gx", "gy", "gz"),
        P("gx", "gy", "gz"),
        P("gx", "gy", "gz"),
        P(),
    )
    return jax.shard_map(
        per_device, mesh=mesh, in_specs=placed, out_specs=P(None, "gx", "gy", "gz"), check_vma=False
    )
```

profile of v0, /device:TPU:97, one launch (start us, length us, event | category | flops | bytes accessed | tf_op | source)
XLA Modules:
  0.0 168.9 jit_solution(4030710210251654959)
XLA Ops:
  3.1 5.0 %select_bitcast_fusion = f32[1,8,8,128]{3,2,1,0:T(8,128)S(1)} fusion(s32[8,8,128]{2,1,0:T(8,128)S(1)} %copy-done.3, f32[]{:T(128)} %bitcast.7, f32[]{:T(128)} %bitcast.6, f32[]{:T(128)} %bitcast.5, f32[]{:T(128)} %bitcast.4, f32[]{:T(128)} %bitcast.3, f32[]{:T(128)} %bitcast.2, f32[]{:T(128)} %bitcast.1, f32[]{:T(128)} %bitcast, ...), kind=kLoop, calls=%fused_computation.883 | loop fusion | flops 212992 | bytes 65712 | tf_op jit(solution)/shard_map/broadcast_in_dim | solution.py:100
  8.1 4.8 %collective-permute-start = (f32[4,1,8,128]{3,2,1,0:T(8,128)S(1)}, f32[4,1,8,128]{3,2,1,0:T(8,128)S(1)}, u32[]{:S(2)}, u32[]{:S(2)}) collective-permute-start(f32[4,1,8,128]{3,2,1,0:T(8,128)S(1)} %get-tuple-element.373), channel_id=1, source_target_pairs={{0,32},{32,64},{64,96},{96,128},{128,160},{160,192},{192,224},{224... | collective-permute-start | bytes 49160 | tf_op jit(solution)/shard_map/ppermute | solution.py:24
  14.8 3.8 %collective-permute-done.1 = f32[4,1,8,128]{3,2,1,0:T(8,128)S(1)} collective-permute-done((f32[4,1,8,128]{3,2,1,0:T(8,128)S(1)}, f32[4,1,8,128]{3,2,1,0:T(8,128)S(1)}, u32[]{:S(2)}, u32[]{:S(2)}) %collective-permute-start.1) | collective-permute-done | bytes 16416 | tf_op jit(solution)/shard_map/ppermute | solution.py:26
  18.7 3.1 %collective-permute-start.2 = (f32[4,10,1,128]{3,2,1,0:T(1,128)S(1)}, f32[4,10,1,128]{3,2,1,0:T(1,128)S(1)}, u32[]{:S(2)}, u32[]{:S(2)}) collective-permute-start(f32[4,10,1,128]{3,2,1,0:T(1,128)S(1)} %get-tuple-element.365), channel_id=1, source_target_pairs={{0,4},{4,8},{8,12},{12,16},{16,20},{20,24},{24,28},{1,5},{5,9},{9,... | collective-permute-start | bytes 61448 | tf_op jit(solution)/shard_map/ppermute | solution.py:24
  23.1 3.2 %collective-permute-done.3 = f32[4,10,1,128]{3,2,1,0:T(1,128)S(1)} collective-permute-done((f32[4,10,1,128]{3,2,1,0:T(1,128)S(1)}, f32[4,10,1,128]{3,2,1,0:T(1,128)S(1)}, u32[]{:S(2)}, u32[]{:S(2)}) %collective-permute-start.3) | collective-permute-done | bytes 20512 | tf_op jit(solution)/shard_map/ppermute | solution.py:26
  26.5 7.8 %collective-permute-start.4 = (f32[4,10,10,1]{3,2,1,0:T(8,128)S(1)}, f32[4,10,10,1]{3,2,1,0:T(8,128)S(1)}, u32[]{:S(2)}, u32[]{:S(2)}) collective-permute-start(f32[4,10,10,1]{3,2,1,0:T(8,128)S(1)} %get-tuple-element.358), channel_id=1, source_target_pairs={{0,1},{1,2},{2,3},{4,5},{5,6},{6,7},{8,9},{9,10},{10,11},{12,13},{... | collective-permute-start | bytes 4808 | tf_op jit(solution)/shard_map/ppermute | solution.py:24
  34.3 1.9 %collective-permute-start.5 = (f32[4,10,10,1]{3,2,1,0:T(8,128)S(1)}, f32[4,10,10,1]{3,2,1,0:T(8,128)S(1)}, u32[]{:S(2)}, u32[]{:S(2)}) collective-permute-start(f32[4,10,10,1]{3,2,1,0:T(8,128)S(1)} %get-tuple-element.357), channel_id=1, source_target_pairs={{1,0},{2,1},{3,2},{5,4},{6,5},{7,6},{9,8},{10,9},{11,10},{13,12},{... | collective-permute-start | bytes 4808 | tf_op jit(solution)/shard_map/ppermute | solution.py:26
  36.2 2.1 %collective-permute-done.4 = f32[4,10,10,1]{3,2,1,0:T(8,128)S(1)} collective-permute-done((f32[4,10,10,1]{3,2,1,0:T(8,128)S(1)}, f32[4,10,10,1]{3,2,1,0:T(8,128)S(1)}, u32[]{:S(2)}, u32[]{:S(2)}) %collective-permute-start.4) | collective-permute-done | bytes 1632 | tf_op jit(solution)/shard_map/ppermute | solution.py:24
  38.3 5.9 %collective-permute-done.5 = f32[4,10,10,1]{3,2,1,0:T(8,128)S(1)} collective-permute-done((f32[4,10,10,1]{3,2,1,0:T(8,128)S(1)}, f32[4,10,10,1]{3,2,1,0:T(8,128)S(1)}, u32[]{:S(2)}, u32[]{:S(2)}) %collective-permute-start.5) | collective-permute-done | bytes 1632 | tf_op jit(solution)/shard_map/ppermute | solution.py:26
  51.9 2.3 %collective-permute-start.6 = (f32[4,1,8,128]{3,2,1,0:T(8,128)S(1)}, f32[4,1,8,128]{3,2,1,0:T(8,128)S(1)}, u32[]{:S(2)}, u32[]{:S(2)}) collective-permute-start(f32[4,1,8,128]{3,2,1,0:T(8,128)S(1)} %get-tuple-element.371), channel_id=1, source_target_pairs={{0,32},{32,64},{64,96},{96,128},{128,160},{160,192},{192,224},{224... | collective-permute-start | bytes 49160 | tf_op jit(solution)/shard_map/ppermute | solution.py:24
  54.2 2.9 %collective-permute-start.7 = (f32[4,1,8,128]{3,2,1,0:T(8,128)S(1)}, f32[4,1,8,128]{3,2,1,0:T(8,128)S(1)}, u32[]{:S(2)}, u32[]{:S(2)}) collective-permute-start(f32[4,1,8,128]{3,2,1,0:T(8,128)S(1)} %get-tuple-element.372), channel_id=1, source_target_pairs={{32,0},{64,32},{96,64},{128,96},{160,128},{192,160},{224,192},{256... | collective-permute-start | bytes 49160 | tf_op jit(solution)/shard_map/ppermute | solution.py:26
  57.2 2.7 %collective-permute-done.7 = f32[4,1,8,128]{3,2,1,0:T(8,128)S(1)} collective-permute-done((f32[4,1,8,128]{3,2,1,0:T(8,128)S(1)}, f32[4,1,8,128]{3,2,1,0:T(8,128)S(1)}, u32[]{:S(2)}, u32[]{:S(2)}) %collective-permute-start.7) | collective-permute-done | bytes 16416 | tf_op jit(solution)/shard_map/ppermute | solution.py:26
  60.0 3.8 %collective-permute-start.8 = (f32[4,10,1,128]{3,2,1,0:T(1,128)S(1)}, f32[4,10,1,128]{3,2,1,0:T(1,128)S(1)}, u32[]{:S(2)}, u32[]{:S(2)}) collective-permute-start(f32[4,10,1,128]{3,2,1,0:T(1,128)S(1)} %get-tuple-element.363), channel_id=1, source_target_pairs={{0,4},{4,8},{8,12},{12,16},{16,20},{20,24},{24,28},{1,5},{5,9},{9,... | collective-permute-start | bytes 61448 | tf_op jit(solution)/shard_map/ppermute | solution.py:24
  65.1 3.2 %collective-permute-done.9 = f32[4,10,1,128]{3,2,1,0:T(1,128)S(1)} collective-permute-done((f32[4,10,1,128]{3,2,1,0:T(1,128)S(1)}, f32[4,10,1,128]{3,2,1,0:T(1,128)S(1)}, u32[]{:S(2)}, u32[]{:S(2)}) %collective-permute-start.9) | collective-permute-done | bytes 20512 | tf_op jit(solution)/shard_map/ppermute | solution.py:26
  68.5 5.2 %collective-permute-start.10 = (f32[4,10,10,1]{3,2,1,0:T(8,128)S(1)}, f32[4,10,10,1]{3,2,1,0:T(8,128)S(1)}, u32[]{:S(2)}, u32[]{:S(2)}) collective-permute-start(f32[4,10,10,1]{3,2,1,0:T(8,128)S(1)} %get-tuple-element.356), channel_id=1, source_target_pairs={{0,1},{1,2},{2,3},{4,5},{5,6},{6,7},{8,9},{9,10},{10,11},{12,13},{... | collective-permute-start | bytes 4808 | tf_op jit(solution)/shard_map/ppermute | solution.py:24
  73.7 2.1 %collective-permute-start.11 = (f32[4,10,10,1]{3,2,1,0:T(8,128)S(1)}, f32[4,10,10,1]{3,2,1,0:T(8,128)S(1)}, u32[]{:S(2)}, u32[]{:S(2)}) collective-permute-start(f32[4,10,10,1]{3,2,1,0:T(8,128)S(1)} %get-tuple-element.355), channel_id=1, source_target_pairs={{1,0},{2,1},{3,2},{5,4},{6,5},{7,6},{9,8},{10,9},{11,10},{13,12},{... | collective-permute-start | bytes 4808 | tf_op jit(solution)/shard_map/ppermute | solution.py:26
  77.7 5.9 %collective-permute-done.11 = f32[4,10,10,1]{3,2,1,0:T(8,128)S(1)} collective-permute-done((f32[4,10,10,1]{3,2,1,0:T(8,128)S(1)}, f32[4,10,10,1]{3,2,1,0:T(8,128)S(1)}, u32[]{:S(2)}, u32[]{:S(2)}) %collective-permute-start.11) | collective-permute-done | bytes 1632 | tf_op jit(solution)/shard_map/ppermute | solution.py:26
  90.4 3.4 %collective-permute-start.12 = (f32[4,1,8,128]{3,2,1,0:T(8,128)S(1)}, f32[4,1,8,128]{3,2,1,0:T(8,128)S(1)}, u32[]{:S(2)}, u32[]{:S(2)}) collective-permute-start(f32[4,1,8,128]{3,2,1,0:T(8,128)S(1)} %get-tuple-element.369), channel_id=1, source_target_pairs={{0,32},{32,64},{64,96},{96,128},{128,160},{160,192},{192,224},{224... | collective-permute-start | bytes 49160 | tf_op jit(solution)/shard_map/ppermute | solution.py:24
  93.8 1.9 %collective-permute-start.13 = (f32[4,1,8,128]{3,2,1,0:T(8,128)S(1)}, f32[4,1,8,128]{3,2,1,0:T(8,128)S(1)}, u32[]{:S(2)}, u32[]{:S(2)}) collective-permute-start(f32[4,1,8,128]{3,2,1,0:T(8,128)S(1)} %get-tuple-element.370), channel_id=1, source_target_pairs={{32,0},{64,32},{96,64},{128,96},{160,128},{192,160},{224,192},{256... | collective-permute-start | bytes 49160 | tf_op jit(solution)/shard_map/ppermute | solution.py:26
  95.7 4.0 %collective-permute-done.13 = f32[4,1,8,128]{3,2,1,0:T(8,128)S(1)} collective-permute-done((f32[4,1,8,128]{3,2,1,0:T(8,128)S(1)}, f32[4,1,8,128]{3,2,1,0:T(8,128)S(1)}, u32[]{:S(2)}, u32[]{:S(2)}) %collective-permute-start.13) | collective-permute-done | bytes 16416 | tf_op jit(solution)/shard_map/ppermute | solution.py:26
  99.8 2.2 %collective-permute-start.14 = (f32[4,10,1,128]{3,2,1,0:T(1,128)S(1)}, f32[4,10,1,128]{3,2,1,0:T(1,128)S(1)}, u32[]{:S(2)}, u32[]{:S(2)}) collective-permute-start(f32[4,10,1,128]{3,2,1,0:T(1,128)S(1)} %get-tuple-element.361), channel_id=1, source_target_pairs={{0,4},{4,8},{8,12},{12,16},{16,20},{20,24},{24,28},{1,5},{5,9},{9,... | collective-permute-start | bytes 61448 | tf_op jit(solution)/shard_map/ppermute | solution.py:24
  103.4 3.9 %collective-permute-done.15 = f32[4,10,1,128]{3,2,1,0:T(1,128)S(1)} collective-permute-done((f32[4,10,1,128]{3,2,1,0:T(1,128)S(1)}, f32[4,10,1,128]{3,2,1,0:T(1,128)S(1)}, u32[]{:S(2)}, u32[]{:S(2)}) %collective-permute-start.15) | collective-permute-done | bytes 20512 | tf_op jit(solution)/shard_map/ppermute | solution.py:26
  107.5 4.2 %collective-permute-start.16 = (f32[4,10,10,1]{3,2,1,0:T(8,128)S(1)}, f32[4,10,10,1]{3,2,1,0:T(8,128)S(1)}, u32[]{:S(2)}, u32[]{:S(2)}) collective-permute-start(f32[4,10,10,1]{3,2,1,0:T(8,128)S(1)} %get-tuple-element.354), channel_id=1, source_target_pairs={{0,1},{1,2},{2,3},{4,5},{5,6},{6,7},{8,9},{9,10},{10,11},{12,13},{... | collective-permute-start | bytes 4808 | tf_op jit(solution)/shard_map/ppermute | solution.py:24
  111.7 2.1 %collective-permute-start.17 = (f32[4,10,10,1]{3,2,1,0:T(8,128)S(1)}, f32[4,10,10,1]{3,2,1,0:T(8,128)S(1)}, u32[]{:S(2)}, u32[]{:S(2)}) collective-permute-start(f32[4,10,10,1]{3,2,1,0:T(8,128)S(1)} %get-tuple-element.353), channel_id=1, source_target_pairs={{1,0},{2,1},{3,2},{5,4},{6,5},{7,6},{9,8},{10,9},{11,10},{13,12},{... | collective-permute-start | bytes 4808 | tf_op jit(solution)/shard_map/ppermute | solution.py:26
  115.7 5.9 %collective-permute-done.17 = f32[4,10,10,1]{3,2,1,0:T(8,128)S(1)} collective-permute-done((f32[4,10,10,1]{3,2,1,0:T(8,128)S(1)}, f32[4,10,10,1]{3,2,1,0:T(8,128)S(1)}, u32[]{:S(2)}, u32[]{:S(2)}) %collective-permute-start.17) | collective-permute-done | bytes 1632 | tf_op jit(solution)/shard_map/ppermute | solution.py:26
  128.5 3.6 %collective-permute-start.18 = (f32[4,1,8,128]{3,2,1,0:T(8,128)S(1)}, f32[4,1,8,128]{3,2,1,0:T(8,128)S(1)}, u32[]{:S(2)}, u32[]{:S(2)}) collective-permute-start(f32[4,1,8,128]{3,2,1,0:T(8,128)S(1)} %get-tuple-element.367), channel_id=1, source_target_pairs={{0,32},{32,64},{64,96},{96,128},{128,160},{160,192},{192,224},{224... | collective-permute-start | bytes 49160 | tf_op jit(solution)/shard_map/ppermute | solution.py:24
  134.1 3.8 %collective-permute-done.19 = f32[4,1,8,128]{3,2,1,0:T(8,128)S(1)} collective-permute-done((f32[4,1,8,128]{3,2,1,0:T(8,128)S(1)}, f32[4,1,8,128]{3,2,1,0:T(8,128)S(1)}, u32[]{:S(2)}, u32[]{:S(2)}) %collective-permute-start.19) | collective-permute-done | bytes 16416 | tf_op jit(solution)/shard_map/ppermute | solution.py:26
  137.9 3.8 %collective-permute-start.20 = (f32[4,10,1,128]{3,2,1,0:T(1,128)S(1)}, f32[4,10,1,128]{3,2,1,0:T(1,128)S(1)}, u32[]{:S(2)}, u32[]{:S(2)}) collective-permute-start(f32[4,10,1,128]{3,2,1,0:T(1,128)S(1)} %get-tuple-element.359), channel_id=1, source_target_pairs={{0,4},{4,8},{8,12},{12,16},{16,20},{20,24},{24,28},{1,5},{5,9},{9,... | collective-permute-start | bytes 61448 | tf_op jit(solution)/shard_map/ppermute | solution.py:24
  142.9 3.2 %collective-permute-done.21 = f32[4,10,1,128]{3,2,1,0:T(1,128)S(1)} collective-permute-done((f32[4,10,1,128]{3,2,1,0:T(1,128)S(1)}, f32[4,10,1,128]{3,2,1,0:T(1,128)S(1)}, u32[]{:S(2)}, u32[]{:S(2)}) %collective-permute-start.21) | collective-permute-done | bytes 20512 | tf_op jit(solution)/shard_map/ppermute | solution.py:26
  146.4 5.2 %collective-permute-start.22 = (f32[4,10,10,1]{3,2,1,0:T(8,128)S(1)}, f32[4,10,10,1]{3,2,1,0:T(8,128)S(1)}, u32[]{:S(2)}, u32[]{:S(2)}) collective-permute-start(f32[4,10,10,1]{3,2,1,0:T(8,128)S(1)} %get-tuple-element.352), channel_id=1, source_target_pairs={{0,1},{1,2},{2,3},{4,5},{5,6},{6,7},{8,9},{9,10},{10,11},{12,13},{... | collective-permute-start | bytes 4808 | tf_op jit(solution)/shard_map/ppermute | solution.py:24
  151.6 2.2 %collective-permute-start.23 = (f32[4,10,10,1]{3,2,1,0:T(8,128)S(1)}, f32[4,10,10,1]{3,2,1,0:T(8,128)S(1)}, u32[]{:S(2)}, u32[]{:S(2)}) collective-permute-start(f32[4,10,10,1]{3,2,1,0:T(8,128)S(1)} %get-tuple-element.351), channel_id=1, source_target_pairs={{1,0},{2,1},{3,2},{5,4},{6,5},{7,6},{9,8},{10,9},{11,10},{13,12},{... | collective-permute-start | bytes 4808 | tf_op jit(solution)/shard_map/ppermute | solution.py:26
  155.6 5.9 %collective-permute-done.23 = f32[4,10,10,1]{3,2,1,0:T(8,128)S(1)} collective-permute-done((f32[4,10,10,1]{3,2,1,0:T(8,128)S(1)}, f32[4,10,10,1]{3,2,1,0:T(8,128)S(1)}, u32[]{:S(2)}, u32[]{:S(2)}) %collective-permute-start.23) | collective-permute-done | bytes 1632 | tf_op jit(solution)/shard_map/ppermute | solution.py:26
  (276 shorter events, 46.0 us)
Async XLA Ops:
  0.0 0.7 copy-start.4
  0.0 1.4 copy-start.2
  2.3 0.8 copy-start.3
  8.1 6.7 %collective-permute-start = (f32[4,1,8,128]{3,2,1,0:T(8,128)S(1)}, f32[4,1,8,128]{3,2,1,0:T(8,128)S(1)}, u32[]{:S(2)}, u32[]{:S(2)}) collective-permute-start(f32[4,1,8,128]{3,2,1,0:T(8,128)S(1)} %get-tuple-element.373), channel_id=1, source_target_pairs={{0,32},{32,64},{64,96},{96,128},{128,160},{160,192},{192,224},{224... | collective-permute-start | bytes 49160 | tf_op jit(solution)/shard_map/ppermute | solution.py:24
  12.9 5.7 %collective-permute-start.1 = (f32[4,1,8,128]{3,2,1,0:T(8,128)S(1)}, f32[4,1,8,128]{3,2,1,0:T(8,128)S(1)}, u32[]{:S(2)}, u32[]{:S(2)}) collective-permute-start(f32[4,1,8,128]{3,2,1,0:T(8,128)S(1)} %get-tuple-element.301), channel_id=1, source_target_pairs={{32,0},{64,32},{96,64},{128,96},{160,128},{192,160},{224,192},{256... | collective-permute-start | bytes 49160 | tf_op jit(solution)/shard_map/ppermute | solution.py:26
  18.7 4.4 %collective-permute-start.2 = (f32[4,10,1,128]{3,2,1,0:T(1,128)S(1)}, f32[4,10,1,128]{3,2,1,0:T(1,128)S(1)}, u32[]{:S(2)}, u32[]{:S(2)}) collective-permute-start(f32[4,10,1,128]{3,2,1,0:T(1,128)S(1)} %get-tuple-element.365), channel_id=1, source_target_pairs={{0,4},{4,8},{8,12},{12,16},{16,20},{20,24},{24,28},{1,5},{5,9},{9,... | collective-permute-start | bytes 61448 | tf_op jit(solution)/shard_map/ppermute | solution.py:24
  21.8 4.5 %collective-permute-start.3 = (f32[4,10,1,128]{3,2,1,0:T(1,128)S(1)}, f32[4,10,1,128]{3,2,1,0:T(1,128)S(1)}, u32[]{:S(2)}, u32[]{:S(2)}) collective-permute-start(f32[4,10,1,128]{3,2,1,0:T(1,128)S(1)} %get-tuple-element.366), channel_id=1, source_target_pairs={{4,0},{8,4},{12,8},{16,12},{20,16},{24,20},{28,24},{5,1},{9,5},{13... | collective-permute-start | bytes 61448 | tf_op jit(solution)/shard_map/ppermute | solution.py:26
  26.5 11.8 %collective-permute-start.4 = (f32[4,10,10,1]{3,2,1,0:T(8,128)S(1)}, f32[4,10,10,1]{3,2,1,0:T(8,128)S(1)}, u32[]{:S(2)}, u32[]{:S(2)}) collective-permute-start(f32[4,10,10,1]{3,2,1,0:T(8,128)S(1)} %get-tuple-element.358), channel_id=1, source_target_pairs={{0,1},{1,2},{2,3},{4,5},{5,6},{6,7},{8,9},{9,10},{10,11},{12,13},{... | collective-permute-start | bytes 4808 | tf_op jit(solution)/shard_map/ppermute | solution.py:24
  34.3 9.9 %collective-permute-start.5 = (f32[4,10,10,1]{3,2,1,0:T(8,128)S(1)}, f32[4,10,10,1]{3,2,1,0:T(8,128)S(1)}, u32[]{:S(2)}, u32[]{:S(2)}) collective-permute-start(f32[4,10,10,1]{3,2,1,0:T(8,128)S(1)} %get-tuple-element.357), channel_id=1, source_target_pairs={{1,0},{2,1},{3,2},{5,4},{6,5},{7,6},{9,8},{10,9},{11,10},{13,12},{... | collective-permute-start | bytes 4808 | tf_op jit(solution)/shard_map/ppermute | solution.py:26
  50.9 0.9 copy-start
  50.9 0.9 copy-start.1
  51.9 5.3 %collective-permute-start.6 = (f32[4,1,8,128]{3,2,1,0:T(8,128)S(1)}, f32[4,1,8,128]{3,2,1,0:T(8,128)S(1)}, u32[]{:S(2)}, u32[]{:S(2)}) collective-permute-start(f32[4,1,8,128]{3,2,1,0:T(8,128)S(1)} %get-tuple-element.371), channel_id=1, source_target_pairs={{0,32},{32,64},{64,96},{96,128},{128,160},{160,192},{192,224},{224... | collective-permute-start | bytes 49160 | tf_op jit(solution)/shard_map/ppermute | solution.py:24
  54.2 5.7 %collective-permute-start.7 = (f32[4,1,8,128]{3,2,1,0:T(8,128)S(1)}, f32[4,1,8,128]{3,2,1,0:T(8,128)S(1)}, u32[]{:S(2)}, u32[]{:S(2)}) collective-permute-start(f32[4,1,8,128]{3,2,1,0:T(8,128)S(1)} %get-tuple-element.372), channel_id=1, source_target_pairs={{32,0},{64,32},{96,64},{128,96},{160,128},{192,160},{224,192},{256... | collective-permute-start | bytes 49160 | tf_op jit(solution)/shard_map/ppermute | solution.py:26
  60.0 5.1 %collective-permute-start.8 = (f32[4,10,1,128]{3,2,1,0:T(1,128)S(1)}, f32[4,10,1,128]{3,2,1,0:T(1,128)S(1)}, u32[]{:S(2)}, u32[]{:S(2)}) collective-permute-start(f32[4,10,1,128]{3,2,1,0:T(1,128)S(1)} %get-tuple-element.363), channel_id=1, source_target_pairs={{0,4},{4,8},{8,12},{12,16},{16,20},{20,24},{24,28},{1,5},{5,9},{9,... | collective-permute-start | bytes 61448 | tf_op jit(solution)/shard_map/ppermute | solution.py:24
  63.7 4.5 %collective-permute-start.9 = (f32[4,10,1,128]{3,2,1,0:T(1,128)S(1)}, f32[4,10,1,128]{3,2,1,0:T(1,128)S(1)}, u32[]{:S(2)}, u32[]{:S(2)}) collective-permute-start(f32[4,10,1,128]{3,2,1,0:T(1,128)S(1)} %get-tuple-element.364), channel_id=1, source_target_pairs={{4,0},{8,4},{12,8},{16,12},{20,16},{24,20},{28,24},{5,1},{9,5},{13... | collective-permute-start | bytes 61448 | tf_op jit(solution)/shard_map/ppermute | solution.py:26
  68.5 9.2 %collective-permute-start.10 = (f32[4,10,10,1]{3,2,1,0:T(8,128)S(1)}, f32[4,10,10,1]{3,2,1,0:T(8,128)S(1)}, u32[]{:S(2)}, u32[]{:S(2)}) collective-permute-start(f32[4,10,10,1]{3,2,1,0:T(8,128)S(1)} %get-tuple-element.356), channel_id=1, source_target_pairs={{0,1},{1,2},{2,3},{4,5},{5,6},{6,7},{8,9},{9,10},{10,11},{12,13},{... | collective-permute-start | bytes 4808 | tf_op jit(solution)/shard_map/ppermute | solution.py:24
  73.7 9.9 %collective-permute-start.11 = (f32[4,10,10,1]{3,2,1,0:T(8,128)S(1)}, f32[4,10,10,1]{3,2,1,0:T(8,128)S(1)}, u32[]{:S(2)}, u32[]{:S(2)}) collective-permute-start(f32[4,10,10,1]{3,2,1,0:T(8,128)S(1)} %get-tuple-element.355), channel_id=1, source_target_pairs={{1,0},{2,1},{3,2},{5,4},{6,5},{7,6},{9,8},{10,9},{11,10},{13,12},{... | collective-permute-start | bytes 4808 | tf_op jit(solution)/shard_map/ppermute | solution.py:26
  90.4 5.3 %collective-permute-start.12 = (f32[4,1,8,128]{3,2,1,0:T(8,128)S(1)}, f32[4,1,8,128]{3,2,1,0:T(8,128)S(1)}, u32[]{:S(2)}, u32[]{:S(2)}) collective-permute-start(f32[4,1,8,128]{3,2,1,0:T(8,128)S(1)} %get-tuple-element.369), channel_id=1, source_target_pairs={{0,32},{32,64},{64,96},{96,128},{128,160},{160,192},{192,224},{224... | collective-permute-start | bytes 49160 | tf_op jit(solution)/shard_map/ppermute | solution.py:24
  93.8 6.0 %collective-permute-start.13 = (f32[4,1,8,128]{3,2,1,0:T(8,128)S(1)}, f32[4,1,8,128]{3,2,1,0:T(8,128)S(1)}, u32[]{:S(2)}, u32[]{:S(2)}) collective-permute-start(f32[4,1,8,128]{3,2,1,0:T(8,128)S(1)} %get-tuple-element.370), channel_id=1, source_target_pairs={{32,0},{64,32},{96,64},{128,96},{160,128},{192,160},{224,192},{256... | collective-permute-start | bytes 49160 | tf_op jit(solution)/shard_map/ppermute | solution.py:26
  99.8 3.5 %collective-permute-start.14 = (f32[4,10,1,128]{3,2,1,0:T(1,128)S(1)}, f32[4,10,1,128]{3,2,1,0:T(1,128)S(1)}, u32[]{:S(2)}, u32[]{:S(2)}) collective-permute-start(f32[4,10,1,128]{3,2,1,0:T(1,128)S(1)} %get-tuple-element.361), channel_id=1, source_target_pairs={{0,4},{4,8},{8,12},{12,16},{16,20},{20,24},{24,28},{1,5},{5,9},{9,... | collective-permute-start | bytes 61448 | tf_op jit(solution)/shard_map/ppermute | solution.py:24
  102.1 5.2 %collective-permute-start.15 = (f32[4,10,1,128]{3,2,1,0:T(1,128)S(1)}, f32[4,10,1,128]{3,2,1,0:T(1,128)S(1)}, u32[]{:S(2)}, u32[]{:S(2)}) collective-permute-start(f32[4,10,1,128]{3,2,1,0:T(1,128)S(1)} %get-tuple-element.362), channel_id=1, source_target_pairs={{4,0},{8,4},{12,8},{16,12},{20,16},{24,20},{28,24},{5,1},{9,5},{13... | collective-permute-start | bytes 61448 | tf_op jit(solution)/shard_map/ppermute | solution.py:26
  107.5 8.2 %collective-permute-start.16 = (f32[4,10,10,1]{3,2,1,0:T(8,128)S(1)}, f32[4,10,10,1]{3,2,1,0:T(8,128)S(1)}, u32[]{:S(2)}, u32[]{:S(2)}) collective-permute-start(f32[4,10,10,1]{3,2,1,0:T(8,128)S(1)} %get-tuple-element.354), channel_id=1, source_target_pairs={{0,1},{1,2},{2,3},{4,5},{5,6},{6,7},{8,9},{9,10},{10,11},{12,13},{... | collective-permute-start | bytes 4808 | tf_op jit(solution)/shard_map/ppermute | solution.py:24
  111.7 9.9 %collective-permute-start.17 = (f32[4,10,10,1]{3,2,1,0:T(8,128)S(1)}, f32[4,10,10,1]{3,2,1,0:T(8,128)S(1)}, u32[]{:S(2)}, u32[]{:S(2)}) collective-permute-start(f32[4,10,10,1]{3,2,1,0:T(8,128)S(1)} %get-tuple-element.353), channel_id=1, source_target_pairs={{1,0},{2,1},{3,2},{5,4},{6,5},{7,6},{9,8},{10,9},{11,10},{13,12},{... | collective-permute-start | bytes 4808 | tf_op jit(solution)/shard_map/ppermute | solution.py:26
  128.5 5.6 %collective-permute-start.18 = (f32[4,1,8,128]{3,2,1,0:T(8,128)S(1)}, f32[4,1,8,128]{3,2,1,0:T(8,128)S(1)}, u32[]{:S(2)}, u32[]{:S(2)}) collective-permute-start(f32[4,1,8,128]{3,2,1,0:T(8,128)S(1)} %get-tuple-element.367), channel_id=1, source_target_pairs={{0,32},{32,64},{64,96},{96,128},{128,160},{160,192},{192,224},{224... | collective-permute-start | bytes 49160 | tf_op jit(solution)/shard_map/ppermute | solution.py:24
  132.1 5.7 %collective-permute-start.19 = (f32[4,1,8,128]{3,2,1,0:T(8,128)S(1)}, f32[4,1,8,128]{3,2,1,0:T(8,128)S(1)}, u32[]{:S(2)}, u32[]{:S(2)}) collective-permute-start(f32[4,1,8,128]{3,2,1,0:T(8,128)S(1)} %get-tuple-element.368), channel_id=1, source_target_pairs={{32,0},{64,32},{96,64},{128,96},{160,128},{192,160},{224,192},{256... | collective-permute-start | bytes 49160 | tf_op jit(solution)/shard_map/ppermute | solution.py:26
  137.9 5.1 %collective-permute-start.20 = (f32[4,10,1,128]{3,2,1,0:T(1,128)S(1)}, f32[4,10,1,128]{3,2,1,0:T(1,128)S(1)}, u32[]{:S(2)}, u32[]{:S(2)}) collective-permute-start(f32[4,10,1,128]{3,2,1,0:T(1,128)S(1)} %get-tuple-element.359), channel_id=1, source_target_pairs={{0,4},{4,8},{8,12},{12,16},{16,20},{20,24},{24,28},{1,5},{5,9},{9,... | collective-permute-start | bytes 61448 | tf_op jit(solution)/shard_map/ppermute | solution.py:24
  141.6 4.5 %collective-permute-start.21 = (f32[4,10,1,128]{3,2,1,0:T(1,128)S(1)}, f32[4,10,1,128]{3,2,1,0:T(1,128)S(1)}, u32[]{:S(2)}, u32[]{:S(2)}) collective-permute-start(f32[4,10,1,128]{3,2,1,0:T(1,128)S(1)} %get-tuple-element.360), channel_id=1, source_target_pairs={{4,0},{8,4},{12,8},{16,12},{20,16},{24,20},{28,24},{5,1},{9,5},{13... | collective-permute-start | bytes 61448 | tf_op jit(solution)/shard_map/ppermute | solution.py:26
  146.4 9.2 %collective-permute-start.22 = (f32[4,10,10,1]{3,2,1,0:T(8,128)S(1)}, f32[4,10,10,1]{3,2,1,0:T(8,128)S(1)}, u32[]{:S(2)}, u32[]{:S(2)}) collective-permute-start(f32[4,10,10,1]{3,2,1,0:T(8,128)S(1)} %get-tuple-element.352), channel_id=1, source_target_pairs={{0,1},{1,2},{2,3},{4,5},{5,6},{6,7},{8,9},{9,10},{10,11},{12,13},{... | collective-permute-start | bytes 4808 | tf_op jit(solution)/shard_map/ppermute | solution.py:24
  151.6 9.9 %collective-permute-start.23 = (f32[4,10,10,1]{3,2,1,0:T(8,128)S(1)}, f32[4,10,10,1]{3,2,1,0:T(8,128)S(1)}, u32[]{:S(2)}, u32[]{:S(2)}) collective-permute-start(f32[4,10,10,1]{3,2,1,0:T(8,128)S(1)} %get-tuple-element.351), channel_id=1, source_target_pairs={{1,0},{2,1},{3,2},{5,4},{6,5},{7,6},{9,8},{10,9},{11,10},{13,12},{... | collective-permute-start | bytes 4808 | tf_op jit(solution)/shard_map/ppermute | solution.py:26
where the time goes:
time: 170 us; the launch traced here: 169 us
  starting transfers between devices  71.6 us (42%)
  waiting for transfers between devices  59.1 us (35%)
  other arithmetic  32.7 us (19%)
  local copies, waits for them, and re-layouts  3.84 us (2%)
  between operations  1.77 us (1%)
    ppermute x12, waiting for transfers between devices, with_halo(): lax.ppermute(head, axis, [((i + 1) % count, i) for i in range(ends)])  51.4 us
    ppermute x12, starting transfers between devices, with_halo(): lax.ppermute(tail, axis, [(i, (i + 1) % count) for i in range(ends)])  49.4 us
    ppermute x12, starting transfers between devices, with_halo(): lax.ppermute(head, axis, [((i + 1) % count, i) for i in range(ends)])  22.2 us
    sub x24, other arithmetic, project(): (1.5 if i == j else 0.0) - 0.5 * sum((rotate[k][i] * rotate[k][j] for k i...  10.1 us
    ppermute x12, waiting for transfers between devices, with_halo(): lax.ppermute(tail, axis, [(i, (i + 1) % count) for i in range(ends)])  7.64 us
    mul x24, other arithmetic, project(): welem * (deform[c][d] - rotate[c][d])  5.75 us
    broadcast_in_dim x1, other arithmetic, node_halo(): joined = jnp.concatenate([disp, weights[None]], axis=0)  5.02 us
    concatenate x16, other arithmetic, with_halo(): jnp.concatenate([lax.ppermute(tail, axis, [(i, (i + 1) % count) for i in...  3.9 us
  transfers between devices with their start and end apart: 24, of which 16 were waited for; matrix products, arithmetic and copies ran while one was open for 0% of the time, Pallas kernels for 0%

commit v1 on v0

v1 whole, which is shorter than its diff:
```python
import functools

import jax
import jax.numpy as jnp
from jax import lax
from jax.experimental import pallas as pl
from jax.experimental.pallas import tpu as pltpu
from jax.sharding import PartitionSpec as P

ITERS = 4
POLAR_STEPS = 6
MATS = 8

relax = 0.6
radius = 0.9

AXES = ("gx", "gy", "gz")
BX = 8
HALO = 2
EX = BX + 2 * HALO
EZ = 128 + 2 * HALO
SLAB = 13
ROWS = 176
VOFF = 16
DIRS = [
    (dx, dy, dz)
    for dx in (-1, 0, 1)
    for dy in (-1, 0, 1)
    for dz in (-1, 0, 1)
    if (dx, dy, dz) != (0, 0, 0)
]


def every(conds):
    conds = [c for c in conds if c is not True]
    return functools.reduce(lambda p, q: p & q, conds) if conds else True


def guarded(cond, act):
    if cond is True:
        act()
    else:
        pl.when(cond)(act)


class Group:
    def __init__(self, width, refs):
        self.h = width
        self.ro, self.ry, self.sy, self.szo, self.szy, self.zo, self.zy, self.ssem, self.rsem = refs
        self.count = self.ro.shape[0]

    @staticmethod
    def scratch(width, count):
        f = jnp.float32
        return [
            pltpu.VMEM((count, EX, BX, 128), f),
            pltpu.VMEM((count, EX, 2, width, 128), f),
            pltpu.VMEM((count, BX, 2, width, 128), f),
            pltpu.VMEM((BX, BX, 128), f),
            pltpu.VMEM((BX, 2, width, 128), f),
            pltpu.VMEM((2, EX, BX, 128), f),
            pltpu.VMEM((2, EX, 2, width, 128), f),
            pltpu.SemaphoreType.DMA((len(DIRS),)),
            pltpu.SemaphoreType.DMA((len(DIRS),)),
        ]

    def copy(self, index, pos):
        dx, dy, dz = DIRS[index]
        h = self.h
        src_x = {-1: (0, h), 0: (0, BX), 1: (BX - h, h)}[dx]
        dst_x = {-1: (HALO + BX, h), 0: (HALO, BX), 1: (HALO - h, h)}[dx]
        src_side, dst_side = {-1: (0, 1), 0: (0, 0), 1: (1, 0)}[dy]
        zside = 0 if dz == 1 else 1
        sx, tx = pl.ds(*src_x), pl.ds(*dst_x)
        if dz == 0:
            if dy == 0:
                src = self.ro.at[:, pl.ds(HALO + src_x[0], src_x[1])]
                dst = self.ro.at[:, tx]
            else:
                src, dst = self.sy.at[:, sx, src_side], self.ry.at[:, tx, dst_side]
        elif dy == 0:
            src, dst = self.szo.at[sx], self.zo.at[zside, tx]
        else:
            src, dst = self.szy.at[sx, src_side], self.zy.at[zside, tx, dst_side]
        return pltpu.make_async_remote_copy(
            src_ref=src,
            dst_ref=dst,
            send_sem=self.ssem.at[index],
            recv_sem=self.rsem.at[index],
            device_id={a: p + d for a, p, d in zip(AXES, pos, DIRS[index])},
            device_id_type=pl.DeviceIdType.MESH,
        )

    def put(self, i, tiles, lane):
        h = self.h
        pack = jnp.zeros_like(tiles[0])
        for c, tile in enumerate(tiles):
            self.ro[c, HALO + i] = tile
            self.sy[c, i, 0] = tile[0:h]
            self.sy[c, i, 1] = tile[BX - h : BX]
            low = pltpu.roll(tile, 4 * c, 1) if c else tile
            high = pltpu.roll(tile, 4 * c + 4, 1)
            inside = (lane >= 4 * c) & (lane < 4 * c + 2)
            pack = jnp.where(inside, low, pack)
            inside = (lane >= 4 * c + 2) & (lane < 4 * c + 4)
            pack = jnp.where(inside, high, pack)
        self.szo[i] = pack
        self.szy[i, 0] = pack[0:h]
        self.szy[i, 1] = pack[BX - h : BX]

    def clear(self, has):
        for d, (start, size) in ((-1, (0, HALO)), (1, (HALO + BX, HALO))):

            def clear_x(start=start, size=size):
                for x in range(start, start + size):
                    for c in range(self.count):
                        self.ro[c, x] = jnp.zeros((BX, 128), jnp.float32)
                        self.ry[c, x] = jnp.zeros(self.ry.shape[2:], jnp.float32)
                    for s in range(2):
                        self.zo[s, x] = jnp.zeros((BX, 128), jnp.float32)
                        self.zy[s, x] = jnp.zeros(self.zy.shape[2:], jnp.float32)

            pl.when(jnp.logical_not(has[0][d]))(clear_x)

            def clear_y(side=(0 if d == -1 else 1)):
                for x in range(EX):
                    for c in range(self.count):
                        self.ry[c, x, side] = jnp.zeros((self.h, 128), jnp.float32)
                    for s in range(2):
                        self.zy[s, x, side] = jnp.zeros((self.h, 128), jnp.float32)

            pl.when(jnp.logical_not(has[1][d]))(clear_y)

            def clear_z(side=(0 if d == -1 else 1)):
                for x in range(EX):
                    self.zo[side, x] = jnp.zeros((BX, 128), jnp.float32)
                    self.zy[side, x] = jnp.zeros(self.zy.shape[2:], jnp.float32)

            pl.when(jnp.logical_not(has[2][d]))(clear_z)

    def send(self, pos, has):
        for index, d in enumerate(DIRS):
            guarded(every([has[a][d[a]] for a in range(3)]), self.copy(index, pos).start)

    def wait_recv(self, pos, has):
        for index, d in enumerate(DIRS):
            guarded(every([has[a][-d[a]] for a in range(3)]), self.copy(index, pos).wait_recv)

    def wait_send(self, pos, has):
        for index, d in enumerate(DIRS):
            guarded(every([has[a][d[a]] for a in range(3)]), self.copy(index, pos).wait_send)

    def to_flat(self, targets):
        h = self.h
        count = self.count
        for part in range(2):
            rows = BX if part == 0 else 2 * h
            lane = lax.broadcasted_iota(jnp.int32, (rows, 128), 1)
            main, zs = (self.ro, self.zo) if part == 0 else (self.ry, self.zy)
            zero = jnp.zeros((rows, 128), jnp.float32)
            before = [zero] * count
            high = zero
            for place in range(SLAB):
                last = place == SLAB - 1
                low = zero if last else zs[0, place].reshape(rows, 128)
                both = jnp.where((lane & 3) < 2, high, low)
                if not last:
                    high = zs[1, place].reshape(rows, 128)
                for c in range(count):
                    now = (
                        zero
                        if last
                        else pltpu.roll(main[c, place].reshape(rows, 128), 4 * place + 2, 1)
                    )
                    ends = pltpu.roll(both, (4 * place - 2 - 4 * c) % 128, 1)
                    flat = jnp.where(
                        lane >= 4 * place + 2,
                        now,
                        jnp.where(lane < 4 * place - 2, before[c], ends),
                    )
                    before[c] = now
                    out = targets[c]
                    if part == 0:
                        out[pl.ds(HALO * SLAB + place, BX, stride=SLAB), :] = flat
                    elif h == 1:
                        out[pl.ds(SLAB + place, 2, stride=9 * SLAB), :] = flat
                    else:
                        out[pl.ds(place, 2, stride=SLAB), :] = flat[0:2]
                        out[pl.ds(10 * SLAB + place, 2, stride=SLAB), :] = flat[2:4]


def own_tile(flat, place, lane):
    start = HALO * SLAB + place
    shift = 4 * place + 2
    first = flat[pl.ds(start, BX, stride=SLAB), :]
    second = flat[pl.ds(start + 1, BX, stride=SLAB), :]
    return pltpu.roll(jnp.where(lane >= shift, first, second), 128 - shift, 1)


def loop(start, rows, step, body):
    trips = -(-rows // step)
    lax.fori_loop(0, trips, lambda t, carry: (body(start + t * step), carry)[1], 0)


def after(ref, row, n, lane, shift):
    whole, part = divmod(shift, 128)
    near = ref[pl.ds(row + whole, n), :]
    far = ref[pl.ds(row + whole + 1, n), :]
    return pltpu.roll(jnp.where(lane < part, far, near), 128 - part, 1)


def earlier(ref, row, n, lane, shift):
    whole, part = divmod(shift, 128)
    near = ref[pl.ds(row - whole, n), :]
    far = ref[pl.ds(row - whole - 1, n), :]
    return pltpu.roll(jnp.where(lane >= 128 - part, far, near), part, 1)


def differences(u, grads, start, rows, n):
    lane = lax.broadcasted_iota(jnp.int32, (n, 128), 1)

    def body(r):
        for c in range(3):
            ref = u.at[c]
            a00 = ref[pl.ds(r, n), :]
            a01 = after(ref, r, n, lane, 1)
            a10 = after(ref, r, n, lane, EZ)
            a11 = after(ref, r, n, lane, EZ + 1)
            s0, s1 = a00 + a01, a10 + a11
            grads[3 * c, pl.ds(r, n), :] = s1 - s0
            grads[3 * c + 1, pl.ds(r, n), :] = s0 + s1
            grads[3 * c + 2, pl.ds(r, n), :] = (a01 - a00) + (a11 - a10)

    loop(start, rows, n, body)


def stresses(grads, weights, corners, spread, start, rows, n):
    def body(r):
        def at(k, row):
            return grads[k, pl.ds(row, n), :]

        deform = []
        for c in range(3):
            fx = at(3 * c, r) + at(3 * c, r + SLAB)
            fy = at(3 * c + 1, r + SLAB) - at(3 * c + 1, r)
            fz = at(3 * c + 2, r) + at(3 * c + 2, r + SLAB)
            deform.append([fx, fy, fz])
        for c in range(3):
            deform[c][c] = deform[c][c] + 1.0
        rows_sq = [
            deform[c][0] * deform[c][0] + deform[c][1] * deform[c][1] + deform[c][2] * deform[c][2]
            for c in range(3)
        ]
        total = rows_sq[0] + rows_sq[1] + rows_sq[2]
        scale = jnp.minimum(lax.rsqrt(total * (2.0 / 3.0)), 0.5**0.5)
        y = [[deform[c][d] * scale for d in range(3)] for c in range(3)]
        weight = weights[pl.ds(r, n), :]
        heavy = weight * 2.0**0.5
        for step in range(POLAR_STEPS):

            def gram(i, j):
                return y[0][i] * y[0][j] + y[1][i] * y[1][j] + y[2][i] * y[2][j]

            d0, d1, d2 = 1.5 - gram(0, 0), 1.5 - gram(1, 1), 1.5 - gram(2, 2)
            o01, o02, o12 = gram(0, 1), gram(0, 2), gram(1, 2)
            if step == POLAR_STEPS - 1:
                d0, d1, d2 = d0 * heavy, d1 * heavy, d2 * heavy
                o01, o02, o12 = o01 * heavy, o02 * heavy, o12 * heavy
            y = [
                [
                    y[c][0] * d0 - (y[c][1] * o01 + y[c][2] * o02),
                    y[c][1] * d1 - (y[c][0] * o01 + y[c][2] * o12),
                    y[c][2] * d2 - (y[c][0] * o02 + y[c][1] * o12),
                ]
                for c in range(3)
            ]
        for c in range(3):
            px, py, pz = (weight * deform[c][d] - y[c][d] for d in range(3))
            s, t = py + px, py - px
            parts = (s + pz, s - pz, t + pz, t - pz)
            for k in range(4):
                corners[4 * c + k, pl.ds(r + VOFF, n), :] = parts[k]
            for k in range(4):
                below = corners[4 * c + k, pl.ds(r + VOFF - SLAB, n), :]
                spread[4 * c + k, pl.ds(r, n), :] = below - parts[3 - k]

    loop(start, rows, n, body)


def update(u, prev, fresh, inertial, rate, spread, omega, start, rows, n):
    lane = lax.broadcasted_iota(jnp.int32, (n, 128), 1)

    def body(r):
        a = rate[pl.ds(r, n), :]
        for c in range(3):
            force = (
                earlier(spread.at[4 * c], r, n, lane, EZ + 1)
                + earlier(spread.at[4 * c + 1], r, n, lane, EZ)
            ) + (
                earlier(spread.at[4 * c + 2], r, n, lane, 1)
                + spread[4 * c + 3, pl.ds(r, n), :]
            )
            here = u[c, pl.ds(r, n), :]
            new = here - a * ((here - inertial[c, pl.ds(r, n), :]) + force)
            if omega is not None:
                old = prev[c, pl.ds(r, n), :]
                new = omega * (new - old) + old
            fresh[c, pl.ds(r, n), :] = new

    loop(start, rows, n, body)


def kernel(
    start_hbm,
    inertial_hbm,
    material_hbm,
    pinned_hbm,
    stiffness,
    out,
    start_v,
    inertial_v,
    material_v,
    pinned_v,
    in_sems,
    ulat,
    wflat,
    iflat,
    pflat,
    rate,
    grads,
    corners,
    spread,
    *group_refs,
):
    pos = [lax.axis_index(a) for a in AXES]
    sizes = [lax.axis_size(a) for a in AXES]
    has = [{-1: p > 0, 0: True, 1: p < n - 1} for p, n in zip(pos, sizes)]
    loads = [
        pltpu.make_async_copy(src, dst, in_sems.at[i])
        for i, (src, dst) in enumerate(
            (
                (start_hbm, start_v),
                (inertial_hbm, inertial_v),
                (material_hbm, material_v),
                (pinned_hbm, pinned_v),
            )
        )
    ]
    for load in loads:
        load.start()
    nine = len(group_refs) // 3
    first = Group(HALO, group_refs[:nine])
    targets = Group(1, group_refs[nine : 2 * nine])
    second = Group(HALO, group_refs[2 * nine :])
    first.clear(has)
    targets.clear(has)

    barrier = pltpu.get_barrier_semaphore()
    for d in DIRS:

        def greet(d=d):
            pl.semaphore_signal(
                barrier,
                inc=1,
                device_id={a: p + e for a, p, e in zip(AXES, pos, d)},
                device_id_type=pl.DeviceIdType.MESH,
            )

        guarded(every([has[a][d[a]] for a in range(3)]), greet)

    for load in loads:
        load.wait()
    lane = lax.broadcasted_iota(jnp.int32, (BX, 128), 1)
    grid_y = lax.broadcasted_iota(jnp.int32, (BX, 128), 0) + pos[1] * BX
    grid_z = lane + pos[2] * 128
    inner = (grid_y < BX * sizes[1] - 1) & (grid_z < 128 * sizes[2] - 1)

    def pack(i, carry):
        pins = pinned_v[i] > 0
        goal = [inertial_v[c, i] * 0.25 for c in range(3)]
        disp = [jnp.where(pins, goal[c], start_v[c, i] * 0.25) for c in range(3)]
        kinds = material_v[i]
        weight = jnp.zeros((BX, 128), jnp.float32)
        for m in range(MATS):
            weight = jnp.where(kinds == m, stiffness[m] * 0.0625, weight)
        valid = inner & (pos[0] * BX + i < BX * sizes[0] - 1)
        first.put(i, disp + [jnp.where(valid, weight, 0.0)], lane)
        targets.put(i, goal + [jnp.where(pins, 1.0, 0.0)], lane)
        return carry

    lax.fori_loop(0, BX, pack, 0)
    sides = [1 + (p > 0).astype(jnp.int32) + (p < n - 1).astype(jnp.int32) for p, n in zip(pos, sizes)]
    pl.semaphore_wait(barrier, sides[0] * sides[1] * sides[2] - 1)
    first.send(pos, has)
    targets.send(pos, has)
    second.clear(has)

    u0, u1, u2 = (ulat.at[k] for k in range(3))
    first.wait_recv(pos, has)
    first.to_flat([u0.at[c] for c in range(3)] + [wflat])

    big = (0, 160, 8), (0, 144, 8), (13, 136, 8)
    small = (13, 136, 8), (13, 120, 8), (26, 104, 8)

    differences(u0, grads, *big[0])
    stresses(grads, wflat, corners, spread, *big[1])

    targets.wait_recv(pos, has)
    targets.to_flat([iflat.at[c] for c in range(3)] + [pflat])

    sums = grads.at[0]

    def layers(r):
        sums[pl.ds(r, 8), :] = wflat[pl.ds(r, 8), :] + wflat[pl.ds(r - SLAB, 8), :]

    loop(SLAB, 136, 8, layers)

    def rates(r):
        total = (earlier(sums, r, 8, lane, EZ + 1) + earlier(sums, r, 8, lane, EZ)) + (
            earlier(sums, r, 8, lane, 1) + sums[pl.ds(r, 8), :]
        )
        rate[pl.ds(r, 8), :] = jnp.where(
            pflat[pl.ds(r, 8), :] > 0.0, 0.0, relax / (1.0 + 3.0 * total)
        )

    loop(SLAB, 136, 8, rates)

    omega1 = 2.0 / (2.0 - radius * radius)
    omega2 = 4.0 / (4.0 - radius * radius * omega1)
    omega3 = 4.0 / (4.0 - radius * radius * omega2)

    update(u0, None, u1, iflat, rate, spread, None, *big[2])
    differences(u1, grads, *small[0])
    stresses(grads, wflat, corners, spread, *small[1])
    update(u1, u0, u2, iflat, rate, spread, omega1, *small[2])

    for i in range(BX):
        second.put(i, [own_tile(u2.at[c], HALO + i, lane) for c in range(3)], lane)
    second.send(pos, has)
    second.wait_recv(pos, has)
    second.to_flat([u2.at[c] for c in range(3)])

    differences(u2, grads, *big[0])
    stresses(grads, wflat, corners, spread, *big[1])
    update(u2, u1, u0, iflat, rate, spread, omega2, *big[2])
    differences(u0, grads, *small[0])
    stresses(grads, wflat, corners, spread, *small[1])
    update(u0, u2, u1, iflat, rate, spread, omega3, *small[2])

    for i in range(BX):
        for c in range(3):
            out[c, i] = 4.0 * own_tile(u1.at[c], HALO + i, lane)
    first.wait_send(pos, has)
    targets.wait_send(pos, has)
    second.wait_send(pos, has)


def per_device(start_disp, inertial, material, pinned, stiffness):
    f = jnp.float32
    flat = (ROWS, 128)
    hbm = pl.BlockSpec(memory_space=pl.ANY)
    return pl.pallas_call(
        kernel,
        out_shape=jax.ShapeDtypeStruct(start_disp.shape, f),
        in_specs=[hbm, hbm, hbm, hbm, pl.BlockSpec(memory_space=pltpu.SMEM)],
        out_specs=pl.BlockSpec(memory_space=pltpu.VMEM),
        scratch_shapes=[
            pltpu.VMEM(start_disp.shape, f),
            pltpu.VMEM(inertial.shape, f),
            pltpu.VMEM(material.shape, jnp.int32),
            pltpu.VMEM(pinned.shape, jnp.int32),
            pltpu.SemaphoreType.DMA((4,)),
            pltpu.VMEM((3, 3, *flat), f),
            pltpu.VMEM(flat, f),
            pltpu.VMEM((3, *flat), f),
            pltpu.VMEM(flat, f),
            pltpu.VMEM(flat, f),
            pltpu.VMEM((9, *flat), f),
            pltpu.VMEM((12, *flat), f),
            pltpu.VMEM((12, *flat), f),
            *Group.scratch(HALO, 4),
            *Group.scratch(1, 4),
            *Group.scratch(HALO, 3),
        ],
        compiler_params=pltpu.CompilerParams(collective_id=0, has_side_effects=True),
    )(start_disp, inertial, material, pinned, stiffness)


def solution(mesh):
    placed = (
        P(None, "gx", "gy", "gz"),
        P(None, "gx", "gy", "gz"),
        P("gx", "gy", "gz"),
        P("gx", "gy", "gz"),
        P(),
    )
    return jax.shard_map(
        per_device, mesh=mesh, in_specs=placed, out_specs=P(None, "gx", "gy", "gz"), check_vma=False
    )
```

time: 170 us -> 42.6 us (0.25)
  the two profiles are of different devices: /device:TPU:97 before, /device:TPU:1 now
where the time goes in v1:
time: 42.6 us; the launch traced here: 42.4 us
  Pallas kernels  40.8 us (96%)
  local copies, waits for them, and re-layouts  1.54 us (4%)
    pallas_call x1, Pallas kernels, per_device(): pl.pallas_call(kernel, out_shape=jax.ShapeDtypeStruct(start_disp.shape, f...  40.8 us
    unnamed x1, local copies, waits for them, and re-layouts  1.54 us

profile of v1, /device:TPU:1, one launch (start us, length us, event | category | flops | bytes accessed | tf_op | source)
XLA Modules:
  0.0 42.4 jit_solution(18227625172268471879)
XLA Ops:
  0.0 40.8 %shard_map.55 = f32[3,8,8,128]{3,2,1,0:T(8,128)} custom-call(f32[3,8,8,128]{3,2,1,0:T(8,128)} %start_hbm.1, f32[3,8,8,128]{3,2,1,0:T(8,128)} %inertial_hbm.1, s32[8,8,128]{2,1,0:T(8,128)} %material_hbm.1, s32[8,8,128]{2,1,0:T(8,128)} %pinned_hbm.1, f32[8]{0:T(128)} %stiffness.1), custom_call_target="tpu_custom_call" | custom-call | tf_op jit(solution)/shard_map/pallas_call | solution.py:462
  40.8 1.5 %copy.7 = f32[3,8,8,128]{3,2,1,0:T(8,128)} copy(f32[3,8,8,128]{3,2,1,0:T(8,128)} %shard_map.55) | data formatting | bytes 196608

commit v2 on v1

--- a/solution.py
+++ b/solution.py
@@ -22,6 +22,7 @@
 SLAB = 13
 ROWS = 176
 VOFF = 16
+ROLLED = 20
 DIRS = [
     (dx, dy, dz)
     for dx in (-1, 0, 1)
@@ -197,9 +198,22 @@
     return pltpu.roll(jnp.where(lane >= shift, first, second), 128 - shift, 1)
 
 
-def loop(start, rows, step, body):
-    trips = -(-rows // step)
-    lax.fori_loop(0, trips, lambda t, carry: (body(start + t * step), carry)[1], 0)
+def loop(start, rows, step, body, unroll=1):
+    blocks = -(-rows // step)
+    unroll = min(unroll, blocks)
+
+    def trip(t, carry):
+        for k in range(unroll):
+            body(start + t * (unroll * step) + k * step)
+        return carry
+
+    trips = blocks // unroll
+    if trips > 1:
+        lax.fori_loop(0, trips, trip, 0)
+    else:
+        trip(0, 0)
+    for k in range(trips * unroll, blocks):
+        body(start + k * step)
 
 
 def after(ref, row, n, lane, shift):
@@ -231,7 +245,7 @@
             grads[3 * c + 1, pl.ds(r, n), :] = s0 + s1
             grads[3 * c + 2, pl.ds(r, n), :] = (a01 - a00) + (a11 - a10)
 
-    loop(start, rows, n, body)
+    loop(start, rows, n, body, ROLLED)
 
 
 def stresses(grads, weights, corners, spread, start, rows, n):
@@ -307,7 +321,7 @@
                 new = omega * (new - old) + old
             fresh[c, pl.ds(r, n), :] = new
 
-    loop(start, rows, n, body)
+    loop(start, rows, n, body, ROLLED)
 
 
 def kernel(
@@ -413,7 +427,7 @@
     def layers(r):
         sums[pl.ds(r, 8), :] = wflat[pl.ds(r, 8), :] + wflat[pl.ds(r - SLAB, 8), :]
 
-    loop(SLAB, 136, 8, layers)
+    loop(SLAB, 136, 8, layers, ROLLED)
 
     def rates(r):
         total = (earlier(sums, r, 8, lane, EZ + 1) + earlier(sums, r, 8, lane, EZ)) + (
@@ -423,7 +437,7 @@
             pflat[pl.ds(r, 8), :] > 0.0, 0.0, relax / (1.0 + 3.0 * total)
         )
 
-    loop(SLAB, 136, 8, rates)
+    loop(SLAB, 136, 8, rates, ROLLED)
 
     omega1 = 2.0 / (2.0 - radius * radius)
     omega2 = 4.0 / (4.0 - radius * radius * omega1)

time: 42.6 us -> 31.3 us (0.73)
  Pallas kernels: 40.8 us -> 29.6 us
    pallas_call x1, Pallas kernels: 40.8 us -> 29.6 us  [per_device(): pl.pallas_call(kernel, out_shape=jax.ShapeDtypeStruct(start_disp.shape, f...]
where the time goes in v2:
time: 31.3 us; the launch traced here: 31.1 us
  Pallas kernels  29.6 us (95%)
  local copies, waits for them, and re-layouts  1.54 us (5%)
    pallas_call x1, Pallas kernels, per_device(): pl.pallas_call(kernel, out_shape=jax.ShapeDtypeStruct(start_disp.shape, f...  29.6 us
    unnamed x1, local copies, waits for them, and re-layouts  1.54 us

profile of v2, /device:TPU:1, one launch (start us, length us, event | category | flops | bytes accessed | tf_op | source)
XLA Modules:
  0.0 31.1 jit_solution(16571380121113095301)
XLA Ops:
  0.0 29.6 %shard_map.55 = f32[3,8,8,128]{3,2,1,0:T(8,128)} custom-call(f32[3,8,8,128]{3,2,1,0:T(8,128)} %start_hbm.1, f32[3,8,8,128]{3,2,1,0:T(8,128)} %inertial_hbm.1, s32[8,8,128]{2,1,0:T(8,128)} %material_hbm.1, s32[8,8,128]{2,1,0:T(8,128)} %pinned_hbm.1, f32[8]{0:T(128)} %stiffness.1), custom_call_target="tpu_custom_call" | custom-call | tf_op jit(solution)/shard_map/pallas_call | solution.py:476
  29.6 1.5 %copy.7 = f32[3,8,8,128]{3,2,1,0:T(8,128)} copy(f32[3,8,8,128]{3,2,1,0:T(8,128)} %shard_map.55) | data formatting | bytes 196608

commit v3 on v2

--- a/solution.py
+++ b/solution.py
@@ -57,10 +57,10 @@
             pltpu.VMEM((count, EX, BX, 128), f),
             pltpu.VMEM((count, EX, 2, width, 128), f),
             pltpu.VMEM((count, BX, 2, width, 128), f),
-            pltpu.VMEM((BX, BX, 128), f),
-            pltpu.VMEM((BX, 2, width, 128), f),
-            pltpu.VMEM((2, EX, BX, 128), f),
-            pltpu.VMEM((2, EX, 2, width, 128), f),
+            pltpu.VMEM((BX, 128), f),
+            pltpu.VMEM((2, width, 128), f),
+            pltpu.VMEM((2, 3, BX, 128), f),
+            pltpu.VMEM((2, 3, 2, width, 128), f),
             pltpu.SemaphoreType.DMA((len(DIRS),)),
             pltpu.SemaphoreType.DMA((len(DIRS),)),
         ]
@@ -72,6 +72,7 @@
         dst_x = {-1: (HALO + BX, h), 0: (HALO, BX), 1: (HALO - h, h)}[dx]
         src_side, dst_side = {-1: (0, 1), 0: (0, 0), 1: (1, 0)}[dy]
         zside = 0 if dz == 1 else 1
+        slot = 1 - dx
         sx, tx = pl.ds(*src_x), pl.ds(*dst_x)
         if dz == 0:
             if dy == 0:
@@ -80,9 +81,9 @@
             else:
                 src, dst = self.sy.at[:, sx, src_side], self.ry.at[:, tx, dst_side]
         elif dy == 0:
-            src, dst = self.szo.at[sx], self.zo.at[zside, tx]
+            src, dst = self.szo, self.zo.at[zside, slot]
         else:
-            src, dst = self.szy.at[sx, src_side], self.zy.at[zside, tx, dst_side]
+            src, dst = self.szy.at[src_side], self.zy.at[zside, slot, dst_side]
         return pltpu.make_async_remote_copy(
             src_ref=src,
             dst_ref=dst,
@@ -92,102 +93,115 @@
             device_id_type=pl.DeviceIdType.MESH,
         )
 
-    def put(self, i, tiles, lane):
+    def put(self, i, tiles, pair, pack):
         h = self.h
-        pack = jnp.zeros_like(tiles[0])
         for c, tile in enumerate(tiles):
             self.ro[c, HALO + i] = tile
             self.sy[c, i, 0] = tile[0:h]
             self.sy[c, i, 1] = tile[BX - h : BX]
-            low = pltpu.roll(tile, 4 * c, 1) if c else tile
-            high = pltpu.roll(tile, 4 * c + 4, 1)
-            inside = (lane >= 4 * c) & (lane < 4 * c + 2)
-            pack = jnp.where(inside, low, pack)
-            inside = (lane >= 4 * c + 2) & (lane < 4 * c + 4)
-            pack = jnp.where(inside, high, pack)
-        self.szo[i] = pack
-        self.szy[i, 0] = pack[0:h]
-        self.szy[i, 1] = pack[BX - h : BX]
+            low = 16 * ((i + 1) % BX) + 4 * c
+            high = 16 * i + 4 * c + 2
+            pack = jnp.where(pair == low // 2, pltpu.roll(tile, low, 1) if low else tile, pack)
+            pack = jnp.where(pair == high // 2, pltpu.roll(tile, (high + 2) % 128, 1), pack)
+        return pack
+
+    def seal(self, pack):
+        h = self.h
+        self.szo[...] = pack
+        self.szy[0] = pack[0:h]
+        self.szy[1] = pack[BX - h : BX]
 
     def clear(self, has):
-        for d, (start, size) in ((-1, (0, HALO)), (1, (HALO + BX, HALO))):
-
-            def clear_x(start=start, size=size):
-                for x in range(start, start + size):
-                    for c in range(self.count):
-                        self.ro[c, x] = jnp.zeros((BX, 128), jnp.float32)
-                        self.ry[c, x] = jnp.zeros(self.ry.shape[2:], jnp.float32)
-                    for s in range(2):
-                        self.zo[s, x] = jnp.zeros((BX, 128), jnp.float32)
-                        self.zy[s, x] = jnp.zeros(self.zy.shape[2:], jnp.float32)
+        h = self.h
+
+        def zero(ref, index):
+            ref[index] = jnp.zeros(ref.at[index].shape, jnp.float32)
+
+        for d in (-1, 1):
+            start = HALO + BX if d == 1 else HALO - h
+            side = 0 if d == -1 else 1
+            slot = 1 + d
+
+            def clear_x(start=start, slot=slot):
+                for c in range(self.count):
+                    for x in range(start, start + h):
+                        zero(self.ro, (c, x))
+                        zero(self.ry, (c, x))
+                for s in range(2):
+                    zero(self.zo, (s, slot))
+                    zero(self.zy, (s, slot))
 
             pl.when(jnp.logical_not(has[0][d]))(clear_x)
 
-            def clear_y(side=(0 if d == -1 else 1)):
-                for x in range(EX):
-                    for c in range(self.count):
-                        self.ry[c, x, side] = jnp.zeros((self.h, 128), jnp.float32)
-                    for s in range(2):
-                        self.zy[s, x, side] = jnp.zeros((self.h, 128), jnp.float32)
+            def clear_y(side=side):
+                for c in range(self.count):
+                    for x in range(EX):
+                        zero(self.ry, (c, x, side))
+                for s in range(2):
+                    for k in range(3):
+                        zero(self.zy, (s, k, side))
 
             pl.when(jnp.logical_not(has[1][d]))(clear_y)
 
-            def clear_z(side=(0 if d == -1 else 1)):
-                for x in range(EX):
-                    self.zo[side, x] = jnp.zeros((BX, 128), jnp.float32)
-                    self.zy[side, x] = jnp.zeros(self.zy.shape[2:], jnp.float32)
+            def clear_z(side=side):
+                for k in range(3):
+                    zero(self.zo, (side, k))
+                    zero(self.zy, (side, k))
 
             pl.when(jnp.logical_not(has[2][d]))(clear_z)
 
     def send(self, pos, has):
+        for index, d in sorted(enumerate(DIRS), key=lambda e: e[1][1] == 0):
+            guarded(every([has[a][d[a]] for a in range(3)]), self.copy(index, pos).start)
+
+    def wait_recv(self, pos, has, edges):
         for index, d in enumerate(DIRS):
-            guarded(every([has[a][d[a]] for a in range(3)]), self.copy(index, pos).start)
-
-    def wait_recv(self, pos, has):
-        for index, d in enumerate(DIRS):
-            guarded(every([has[a][-d[a]] for a in range(3)]), self.copy(index, pos).wait_recv)
+            if (d[1] != 0) == edges:
+                guarded(every([has[a][-d[a]] for a in range(3)]), self.copy(index, pos).wait_recv)
 
     def wait_send(self, pos, has):
         for index, d in enumerate(DIRS):
             guarded(every([has[a][d[a]] for a in range(3)]), self.copy(index, pos).wait_send)
 
-    def to_flat(self, targets):
+    def to_flat(self, targets, edges):
         h = self.h
         count = self.count
-        for part in range(2):
-            rows = BX if part == 0 else 2 * h
-            lane = lax.broadcasted_iota(jnp.int32, (rows, 128), 1)
-            main, zs = (self.ro, self.zo) if part == 0 else (self.ry, self.zy)
-            zero = jnp.zeros((rows, 128), jnp.float32)
-            before = [zero] * count
-            high = zero
-            for place in range(SLAB):
-                last = place == SLAB - 1
-                low = zero if last else zs[0, place].reshape(rows, 128)
-                both = jnp.where((lane & 3) < 2, high, low)
-                if not last:
-                    high = zs[1, place].reshape(rows, 128)
-                for c in range(count):
-                    now = (
-                        zero
-                        if last
-                        else pltpu.roll(main[c, place].reshape(rows, 128), 4 * place + 2, 1)
-                    )
-                    ends = pltpu.roll(both, (4 * place - 2 - 4 * c) % 128, 1)
-                    flat = jnp.where(
-                        lane >= 4 * place + 2,
-                        now,
-                        jnp.where(lane < 4 * place - 2, before[c], ends),
-                    )
-                    before[c] = now
-                    out = targets[c]
-                    if part == 0:
-                        out[pl.ds(HALO * SLAB + place, BX, stride=SLAB), :] = flat
-                    elif h == 1:
-                        out[pl.ds(SLAB + place, 2, stride=9 * SLAB), :] = flat
-                    else:
-                        out[pl.ds(place, 2, stride=SLAB), :] = flat[0:2]
-                        out[pl.ds(10 * SLAB + place, 2, stride=SLAB), :] = flat[2:4]
+        rows = 2 * h if edges else BX
+        lane = lax.broadcasted_iota(jnp.int32, (rows, 128), 1)
+        main, zs = (self.ry, self.zy) if edges else (self.ro, self.zo)
+        zero = jnp.zeros((rows, 128), jnp.float32)
+        low_z, high_z = ([zs[s, k].reshape(rows, 128) for k in range(3)] for s in range(2))
+        before = [zero] * count
+        for place in range(SLAB):
+            first, last = place == 0, place == SLAB - 1
+            slot, before_slot = ((p >= HALO) + (p >= HALO + BX) for p in (place, place - 1))
+            base = 16 * ((place - HALO) % BX)
+            both = jnp.where(
+                (lane & 3) < 2,
+                zero if first else high_z[before_slot],
+                zero if last else low_z[slot],
+            )
+            for c in range(count):
+                now = (
+                    zero
+                    if last
+                    else pltpu.roll(main[c, place].reshape(rows, 128), 4 * place + 2, 1)
+                )
+                ends = pltpu.roll(both, (4 * place - 2 - 4 * c - base) % 128, 1)
+                flat = jnp.where(
+                    lane >= 4 * place + 2,
+                    now,
+                    jnp.where(lane < 4 * place - 2, before[c], ends),
+                )
+                before[c] = now
+                out = targets[c]
+                if not edges:
+                    out[pl.ds(HALO * SLAB + place, BX, stride=SLAB), :] = flat
+                elif h == 1:
+                    out[pl.ds(SLAB + place, 2, stride=9 * SLAB), :] = flat
+                else:
+                    out[pl.ds(place, 2, stride=SLAB), :] = flat[0:2]
+                    out[pl.ds(10 * SLAB + place, 2, stride=SLAB), :] = flat[2:4]
 
 
 def own_tile(flat, place, lane):
@@ -299,6 +313,13 @@
                 spread[4 * c + k, pl.ds(r, n), :] = below - parts[3 - k]
 
     loop(start, rows, n, body)
+
+
+def respread(corners, spread, row):
+    for c in range(3):
+        for k in range(4):
+            below = corners[4 * c + k, pl.ds(row + VOFF - SLAB, 8), :]
+            spread[4 * c + k, pl.ds(row, 8), :] = below - corners[4 * c + 3 - k, pl.ds(row + VOFF, 8), :]
 
 
 def update(u, prev, fresh, inertial, rate, spread, omega, start, rows, n):
@@ -366,11 +387,8 @@
     first = Group(HALO, group_refs[:nine])
     targets = Group(1, group_refs[nine : 2 * nine])
     second = Group(HALO, group_refs[2 * nine :])
-    first.clear(has)
-    targets.clear(has)
-
     barrier = pltpu.get_barrier_semaphore()
-    for d in DIRS:
+    for d in sorted(DIRS, key=lambda e: -sum(map(abs, e))):
 
         def greet(d=d):
             pl.semaphore_signal(
@@ -381,6 +399,8 @@
             )
 
         guarded(every([has[a][d[a]] for a in range(3)]), greet)
+    first.clear(has)
+    targets.clear(has)
 
     for load in loads:
         load.wait()
@@ -389,20 +409,23 @@
     grid_z = lane + pos[2] * 128
     inner = (grid_y < BX * sizes[1] - 1) & (grid_z < 128 * sizes[2] - 1)
 
-    def pack(i, carry):
+    pair = lane >> 1
+    zero = jnp.zeros((BX, 128), jnp.float32)
+    packs = [zero, zero]
+    for i in range(BX):
         pins = pinned_v[i] > 0
         goal = [inertial_v[c, i] * 0.25 for c in range(3)]
         disp = [jnp.where(pins, goal[c], start_v[c, i] * 0.25) for c in range(3)]
         kinds = material_v[i]
-        weight = jnp.zeros((BX, 128), jnp.float32)
+        weight = zero
         for m in range(MATS):
             weight = jnp.where(kinds == m, stiffness[m] * 0.0625, weight)
         valid = inner & (pos[0] * BX + i < BX * sizes[0] - 1)
-        first.put(i, disp + [jnp.where(valid, weight, 0.0)], lane)
-        targets.put(i, goal + [jnp.where(pins, 1.0, 0.0)], lane)
-        return carry
-
-    lax.fori_loop(0, BX, pack, 0)
+        packs[0] = first.put(i, disp + [jnp.where(valid, weight, 0.0)], pair, packs[0])
+        packs[1] = targets.put(i, goal + [jnp.where(pins, 1.0, 0.0)], pair, packs[1])
+    first.seal(packs[0])
+    targets.seal(packs[1])
+
     sides = [1 + (p > 0).astype(jnp.int32) + (p < n - 1).astype(jnp.int32) for p, n in zip(pos, sizes)]
     pl.semaphore_wait(barrier, sides[0] * sides[1] * sides[2] - 1)
     first.send(pos, has)
@@ -410,17 +433,27 @@
     second.clear(has)
 
     u0, u1, u2 = (ulat.at[k] for k in range(3))
-    first.wait_recv(pos, has)
-    first.to_flat([u0.at[c] for c in range(3)] + [wflat])
-
-    big = (0, 160, 8), (0, 144, 8), (13, 136, 8)
     small = (13, 136, 8), (13, 120, 8), (26, 104, 8)
-
-    differences(u0, grads, *big[0])
-    stresses(grads, wflat, corners, spread, *big[1])
-
-    targets.wait_recv(pos, has)
-    targets.to_flat([iflat.at[c] for c in range(3)] + [pflat])
+    firsts = [u0.at[c] for c in range(3)] + [wflat]
+    goals = [iflat.at[c] for c in range(3)] + [pflat]
+
+    def wide(group, targets, u):
+        group.wait_recv(pos, has, False)
+        group.to_flat(targets, False)
+        differences(u, grads, 26, 104, 8)
+        stresses(grads, wflat, corners, spread, 26, 88, 8)
+        group.wait_recv(pos, has, True)
+        group.to_flat(targets, True)
+        differences(u, grads, 0, 32, 8)
+        differences(u, grads, 130, 32, 8)
+        stresses(grads, wflat, corners, spread, 0, 32, 8)
+        stresses(grads, wflat, corners, spread, 114, 32, 8)
+        respread(corners, spread, 32)
+
+    wide(first, firsts, u0)
+    for edges in (False, True):
+        targets.wait_recv(pos, has, edges)
+        targets.to_flat(goals, edges)
 
     sums = grads.at[0]
 
@@ -443,20 +476,18 @@
     omega2 = 4.0 / (4.0 - radius * radius * omega1)
     omega3 = 4.0 / (4.0 - radius * radius * omega2)
 
-    update(u0, None, u1, iflat, rate, spread, None, *big[2])
+    update(u0, None, u1, iflat, rate, spread, None, SLAB, 136, 8)
     differences(u1, grads, *small[0])
     stresses(grads, wflat, corners, spread, *small[1])
     update(u1, u0, u2, iflat, rate, spread, omega1, *small[2])
 
+    pack = zero
     for i in range(BX):
-        second.put(i, [own_tile(u2.at[c], HALO + i, lane) for c in range(3)], lane)
+        pack = second.put(i, [own_tile(u2.at[c], HALO + i, lane) for c in range(3)], pair, pack)
+    second.seal(pack)
     second.send(pos, has)
-    second.wait_recv(pos, has)
-    second.to_flat([u2.at[c] for c in range(3)])
-
-    differences(u2, grads, *big[0])
-    stresses(grads, wflat, corners, spread, *big[1])
-    update(u2, u1, u0, iflat, rate, spread, omega2, *big[2])
+    wide(second, [u2.at[c] for c in range(3)], u2)
+    update(u2, u1, u0, iflat, rate, spread, omega2, SLAB, 136, 8)
     differences(u0, grads, *small[0])
     stresses(grads, wflat, corners, spread, *small[1])
     update(u0, u2, u1, iflat, rate, spread, omega3, *small[2])

time: 31.3 us -> 30.5 us (0.974)
  the two profiles are of different devices: /device:TPU:1 before, /device:TPU:121 now
where the time goes in v3:
time: 30.5 us; the launch traced here: 30.3 us
  Pallas kernels  28.8 us (94%)
  local copies, waits for them, and re-layouts  1.54 us (5%)
    pallas_call x1, Pallas kernels, per_device(): pl.pallas_call(kernel, out_shape=jax.ShapeDtypeStruct(start_disp.shape, f...  28.8 us
    unnamed x1, local copies, waits for them, and re-layouts  1.54 us

profile of v3, /device:TPU:121, one launch (start us, length us, event | category | flops | bytes accessed | tf_op | source)
XLA Modules:
  0.0 30.3 jit_solution(13754662583012347195)
XLA Ops:
  0.0 28.8 %shard_map.55 = f32[3,8,8,128]{3,2,1,0:T(8,128)} custom-call(f32[3,8,8,128]{3,2,1,0:T(8,128)} %start_hbm.1, f32[3,8,8,128]{3,2,1,0:T(8,128)} %inertial_hbm.1, s32[8,8,128]{2,1,0:T(8,128)} %material_hbm.1, s32[8,8,128]{2,1,0:T(8,128)} %pinned_hbm.1, f32[8]{0:T(128)} %stiffness.1), custom_call_target="tpu_custom_call" | custom-call | tf_op jit(solution)/shard_map/pallas_call | solution.py:507
  28.8 1.5 %copy.7 = f32[3,8,8,128]{3,2,1,0:T(8,128)} copy(f32[3,8,8,128]{3,2,1,0:T(8,128)} %shard_map.55) | data formatting | bytes 196608

commit v4 on v3

v4 whole, which is shorter than its diff:
```python
import functools

import jax
import jax.numpy as jnp
from jax import lax
from jax.experimental import pallas as pl
from jax.experimental.pallas import tpu as pltpu
from jax.sharding import PartitionSpec as P

ITERS = 4
POLAR_STEPS = 6
MATS = 8

relax = 0.6
radius = 0.9

AXES = ("gx", "gy", "gz")
BX = 8
HALO = 2
EX = BX + 2 * HALO
HZ = 2 * HALO
EZ = 128 + 2 * HZ
SLAB = 13
ROWS = 176
VOFF = 16
ROLLED = 20
DIRS = [
    (dx, dy, dz)
    for dx in (-1, 0, 1)
    for dy in (-1, 0, 1)
    for dz in (-1, 0, 1)
    if (dx, dy, dz) != (0, 0, 0)
]


def every(conds):
    conds = [c for c in conds if c is not True]
    return functools.reduce(lambda p, q: p & q, conds) if conds else True


def guarded(cond, act):
    if cond is True:
        act()
    else:
        pl.when(cond)(act)


class Group:
    def __init__(self, width, dz, refs):
        self.h = width
        self.dz = dz
        self.ro, self.ry, self.sy, self.szo, self.szy, self.zo, self.zy, self.ssem, self.rsem = refs
        self.count = self.ro.shape[0]
        if dz:
            self.messages = list(DIRS)
        else:
            flat = [d for d in DIRS if d[2] == 0]
            self.messages = flat + [(*d[:2], None) for d in flat]

    @staticmethod
    def scratch(width, dz, count):
        f = jnp.float32
        sides = 2 if dz else 1
        total = len(DIRS) if dz else 16
        return [
            pltpu.VMEM((count, EX, BX, 128), f),
            pltpu.VMEM((count, EX, 2, width, 128), f),
            pltpu.VMEM((count, BX, 2, width, 128), f),
            pltpu.VMEM((2, BX, 128), f),
            pltpu.VMEM((2, 2, width, 128), f),
            pltpu.VMEM((sides, 3, 2, BX, 128), f),
            pltpu.VMEM((sides, 3, 2, 2, width, 128), f),
            pltpu.SemaphoreType.DMA((total,)),
            pltpu.SemaphoreType.DMA((total,)),
        ]

    def copy(self, index, pos):
        dx, dy, dz = self.messages[index]
        h = self.h
        src_x = {-1: (0, h), 0: (0, BX), 1: (BX - h, h)}[dx]
        dst_x = {-1: (HALO + BX, h), 0: (HALO, BX), 1: (HALO - h, h)}[dx]
        src_side, dst_side = {-1: (0, 1), 0: (0, 0), 1: (1, 0)}[dy]
        zside = 1 if dz == -1 else 0
        slot = 1 - dx
        sx, tx = pl.ds(*src_x), pl.ds(*dst_x)
        if dz == 0:
            if dy == 0:
                src = self.ro.at[:, pl.ds(HALO + src_x[0], src_x[1])]
                dst = self.ro.at[:, tx]
            else:
                src, dst = self.sy.at[:, sx, src_side], self.ry.at[:, tx, dst_side]
        elif dy == 0:
            src, dst = self.szo, self.zo.at[zside, slot]
        else:
            src, dst = self.szy.at[:, src_side], self.zy.at[zside, slot, :, dst_side]
        return pltpu.make_async_remote_copy(
            src_ref=src,
            dst_ref=dst,
            send_sem=self.ssem.at[index],
            recv_sem=self.rsem.at[index],
            device_id={a: p + d for a, p, d in zip(AXES, pos, (dx, dy, dz or 0))},
            device_id_type=pl.DeviceIdType.MESH,
        )

    def put(self, i, tiles):
        h = self.h
        for c, tile in enumerate(tiles):
            self.ro[c, HALO + i] = tile
            self.sy[c, i, 0] = tile[0:h]
            self.sy[c, i, 1] = tile[BX - h : BX]

    def seal(self, packs):
        h = self.h
        for k, pack in enumerate(packs):
            self.szo[k] = pack
            self.szy[k, 0] = pack[0:h]
            self.szy[k, 1] = pack[BX - h : BX]

    def clear(self, has):
        h = self.h
        zsides = self.zo.shape[0]

        def zero(ref, index):
            ref[index] = jnp.zeros(ref.at[index].shape, jnp.float32)

        for d in (-1, 1):
            start = HALO + BX if d == 1 else HALO - h
            side = 0 if d == -1 else 1
            slot = 1 + d

            def clear_x(start=start, slot=slot):
                for c in range(self.count):
                    for x in range(start, start + h):
                        zero(self.ro, (c, x))
                        zero(self.ry, (c, x))
                for s in range(zsides):
                    for k in range(2):
                        zero(self.zo, (s, slot, k))
                        zero(self.zy, (s, slot, k))

            pl.when(jnp.logical_not(has[0][d]))(clear_x)

            def clear_y(side=side):
                for c in range(self.count):
                    for x in range(EX):
                        zero(self.ry, (c, x, side))
                for s in range(zsides):
                    for slot in range(3):
                        for k in range(2):
                            zero(self.zy, (s, slot, k, side))

            pl.when(jnp.logical_not(has[1][d]))(clear_y)

            def clear_z(side=side):
                for slot in range(3):
                    for k in range(2):
                        zero(self.zo, (side, slot, k))
                        zero(self.zy, (side, slot, k))

            if self.dz:
                pl.when(jnp.logical_not(has[2][d]))(clear_z)

    def send(self, pos, has):
        for index, d in sorted(enumerate(self.messages), key=lambda e: e[1][1] == 0):
            guarded(every([has[a][d[a] or 0] for a in range(3)]), self.copy(index, pos).start)

    def wait_recv(self, pos, has, edges):
        for index, d in enumerate(self.messages):
            if (d[1] != 0) == edges:
                there = every([has[a][-(d[a] or 0)] for a in range(3)])
                guarded(there, self.copy(index, pos).wait_recv)

    def wait_send(self, pos, has):
        for index, d in enumerate(self.messages):
            guarded(every([has[a][d[a] or 0] for a in range(3)]), self.copy(index, pos).wait_send)

    def to_flat(self, targets, edges):
        h = self.h
        count = self.count
        rows = 2 * h if edges else BX
        lane = lax.broadcasted_iota(jnp.int32, (rows, 128), 1)
        main, zs = (self.ry, self.zy) if edges else (self.ro, self.zo)
        zero = jnp.zeros((rows, 128), jnp.float32)
        kept = not (edges or self.dz)
        before = [zero] * count
        for place in range(SLAB):
            if kept and HALO < place < HALO + BX:
                continue
            first, last = place == 0, place == SLAB - 1
            slot, before_slot = ((p >= HALO) + (p >= HALO + BX) for p in (place, place - 1))
            unit = (place - HALO) % BX

            def columns(side, slot):
                if kept and slot == 1:
                    return zero
                return zs[side, slot, unit // 4].reshape(rows, 128)

            both = jnp.where(
                (lane & 7) < HZ,
                zero if first else columns(zs.shape[0] - 1, before_slot),
                zero if last else columns(0, slot),
            )
            for c in range(count):
                if last or (kept and slot == 1):
                    now = zero
                else:
                    now = pltpu.roll(main[c, place].reshape(rows, 128), 8 * place + HZ, 1)
                ends = pltpu.roll(both, (8 * place - HZ - 32 * (unit % 4) - 8 * c) % 128, 1)
                flat = jnp.where(
                    lane >= 8 * place + HZ,
                    now,
                    jnp.where(lane < 8 * place - HZ, before[c], ends),
                )
                before[c] = now
                out = targets[c]
                if not edges:
                    span = pl.ds(HALO * SLAB + place, BX, stride=SLAB)
                    if kept and place == HALO:
                        flat = jnp.where(lane < 8 * place, flat, out[span, :])
                    if kept and place == HALO + BX:
                        flat = jnp.where(lane < 8 * place, out[span, :], flat)
                    out[span, :] = flat
                elif h == 1:
                    out[pl.ds(SLAB + place, 2, stride=9 * SLAB), :] = flat
                else:
                    out[pl.ds(place, 2, stride=SLAB), :] = flat[0:2]
                    out[pl.ds(10 * SLAB + place, 2, stride=SLAB), :] = flat[2:4]


def merge(packs, unit, field, half, tile, lane4, from_lane):
    to = 32 * (unit % 4) + 8 * field + 4 * half
    shift = (to - from_lane) % 128
    moved = pltpu.roll(tile, shift, 1) if shift else tile
    packs[unit // 4] = jnp.where(lane4 == to // 4, moved, packs[unit // 4])


def pack_block(packs, i, tiles, lane4):
    for c, tile in enumerate(tiles):
        merge(packs, (i + 1) % BX, c, 0, tile, lane4, 0)
        merge(packs, i, c, 1, tile, lane4, 128 - HZ)


def loop(start, rows, step, body, unroll=1):
    blocks = -(-rows // step)
    unroll = min(unroll, blocks)

    def trip(t, carry):
        for k in range(unroll):
            body(start + t * (unroll * step) + k * step)
        return carry

    trips = blocks // unroll
    if trips > 1:
        lax.fori_loop(0, trips, trip, 0)
    else:
        trip(0, 0)
    for k in range(trips * unroll, blocks):
        body(start + k * step)


def span(row, stride):
    return pl.ds(row, 8) if stride == 1 else pl.ds(row, 8, stride=stride)


def after(ref, row, stride, lane, shift):
    whole, part = divmod(shift, 128)
    near = ref[span(row + whole, stride), :]
    far = ref[span(row + whole + 1, stride), :]
    return pltpu.roll(jnp.where(lane < part, far, near), 128 - part, 1)


def earlier(get, row, lane, shift):
    whole, part = divmod(shift, 128)
    return pltpu.roll(jnp.where(lane >= 128 - part, get(row - whole - 1), get(row - whole)), part, 1)


def differences(u, grads, lane, row, stride=1):
    for c in range(3):
        ref = u.at[c]
        a00 = ref[span(row, stride), :]
        a01 = after(ref, row, stride, lane, 1)
        a10 = after(ref, row, stride, lane, EZ)
        a11 = after(ref, row, stride, lane, EZ + 1)
        s0, s1 = a00 + a01, a10 + a11
        grads[3 * c, span(row, stride), :] = s1 - s0
        grads[3 * c + 1, span(row, stride), :] = s0 + s1
        grads[3 * c + 2, span(row, stride), :] = (a01 - a00) + (a11 - a10)


def stresses(grads, weights, corners, row, stride=1):
    def at(k, r):
        return grads[k, span(r, stride), :]

    deform = []
    for c in range(3):
        fx = at(3 * c, row) + at(3 * c, row + SLAB)
        fy = at(3 * c + 1, row + SLAB) - at(3 * c + 1, row)
        fz = at(3 * c + 2, row) + at(3 * c + 2, row + SLAB)
        deform.append([fx, fy, fz])
    for c in range(3):
        deform[c][c] = deform[c][c] + 1.0
    rows_sq = [
        deform[c][0] * deform[c][0] + deform[c][1] * deform[c][1] + deform[c][2] * deform[c][2]
        for c in range(3)
    ]
    total = rows_sq[0] + rows_sq[1] + rows_sq[2]
    scale = jnp.minimum(lax.rsqrt(total * (2.0 / 3.0)), 0.5**0.5)
    y = [[deform[c][d] * scale for d in range(3)] for c in range(3)]
    weight = weights[span(row, stride), :]
    heavy = weight * 2.0**0.5
    for step in range(POLAR_STEPS):

        def gram(i, j):
            return y[0][i] * y[0][j] + y[1][i] * y[1][j] + y[2][i] * y[2][j]

        d0, d1, d2 = 1.5 - gram(0, 0), 1.5 - gram(1, 1), 1.5 - gram(2, 2)
        o01, o02, o12 = gram(0, 1), gram(0, 2), gram(1, 2)
        if step == POLAR_STEPS - 1:
            d0, d1, d2 = d0 * heavy, d1 * heavy, d2 * heavy
            o01, o02, o12 = o01 * heavy, o02 * heavy, o12 * heavy
        y = [
            [
                y[c][0] * d0 - (y[c][1] * o01 + y[c][2] * o02),
                y[c][1] * d1 - (y[c][0] * o01 + y[c][2] * o12),
                y[c][2] * d2 - (y[c][0] * o02 + y[c][1] * o12),
            ]
            for c in range(3)
        ]
    for c in range(3):
        px, py, pz = (weight * deform[c][d] - y[c][d] for d in range(3))
        s, t = py + px, py - px
        for k, part in enumerate((s + pz, s - pz, t + pz, t - pz)):
            corners[4 * c + k, span(row + VOFF, stride), :] = part


def update(state, u, prev, inertial, rate, corners, omega, lane, row, stride=1):
    seen = state.setdefault(stride, {})

    def spread(c, k):
        def get(r):
            if (c, k, r) not in seen:
                below = corners[4 * c + k, span(r + VOFF - SLAB, stride), :]
                seen[c, k, r] = below - corners[4 * c + 3 - k, span(r + VOFF, stride), :]
            return seen[c, k, r]

        return get

    a = rate[span(row, stride), :]
    result = []
    for c in range(3):
        force = (
            earlier(spread(c, 0), row, lane, EZ + 1) + earlier(spread(c, 1), row, lane, EZ)
        ) + (earlier(spread(c, 2), row, lane, 1) + spread(c, 3)(row))
        here = u[c, span(row, stride), :]
        new = here - a * ((here - inertial[c, span(row, stride), :]) + force)
        if omega is not None:
            old = prev[c, span(row, stride), :]
            new = omega * (new - old) + old
        result.append(new)
    return result


def kernel(
    start_hbm,
    inertial_hbm,
    material_hbm,
    pinned_hbm,
    stiffness,
    out,
    start_v,
    inertial_v,
    material_v,
    pinned_v,
    in_sems,
    ulat,
    wflat,
    iflat,
    pflat,
    rate,
    grads,
    corners,
    *group_refs,
):
    pos = [lax.axis_index(a) for a in AXES]
    sizes = [lax.axis_size(a) for a in AXES]
    has = [{-1: p > 0, 0: True, 1: p < n - 1} for p, n in zip(pos, sizes)]
    loads = [
        pltpu.make_async_copy(src, dst, in_sems.at[i])
        for i, (src, dst) in enumerate(
            (
                (start_hbm, start_v),
                (inertial_hbm, inertial_v),
                (material_hbm, material_v),
                (pinned_hbm, pinned_v),
            )
        )
    ]
    for load in loads:
        load.start()
    nine = len(group_refs) // 3
    first = Group(HALO, True, group_refs[:nine])
    targets = Group(1, True, group_refs[nine : 2 * nine])
    second = Group(HALO, False, group_refs[2 * nine :])
    barrier = pltpu.get_barrier_semaphore()
    for d in sorted(DIRS, key=lambda e: -sum(map(abs, e))):

        def greet(d=d):
            pl.semaphore_signal(
                barrier,
                inc=1,
                device_id={a: p + e for a, p, e in zip(AXES, pos, d)},
                device_id_type=pl.DeviceIdType.MESH,
            )

        guarded(every([has[a][d[a]] for a in range(3)]), greet)
    first.clear(has)
    targets.clear(has)

    for load in loads:
        load.wait()
    lane = lax.broadcasted_iota(jnp.int32, (BX, 128), 1)
    grid_y = lax.broadcasted_iota(jnp.int32, (BX, 128), 0) + pos[1] * BX
    grid_z = lane + pos[2] * 128
    inner = (grid_y < BX * sizes[1] - 1) & (grid_z < 128 * sizes[2] - 1)

    lane4 = lane >> 2
    zero = jnp.zeros((BX, 128), jnp.float32)
    packs = [[zero, zero], [zero, zero]]
    for i in range(BX):
        pins = pinned_v[i] > 0
        goal = [inertial_v[c, i] * 0.25 for c in range(3)]
        disp = [jnp.where(pins, goal[c], start_v[c, i] * 0.25) for c in range(3)]
        kinds = material_v[i]
        weight = zero
        for m in range(MATS):
            weight = jnp.where(kinds == m, stiffness[m] * 0.0625, weight)
        valid = inner & (pos[0] * BX + i < BX * sizes[0] - 1)
        fields = (disp + [jnp.where(valid, weight, 0.0)], goal + [jnp.where(pins, 1.0, 0.0)])
        for group, pack, tiles in zip((first, targets), packs, fields):
            group.put(i, tiles)
            pack_block(pack, i, tiles, lane4)
    first.seal(packs[0])
    targets.seal(packs[1])

    sides = [1 + (p > 0).astype(jnp.int32) + (p < n - 1).astype(jnp.int32) for p, n in zip(pos, sizes)]
    pl.semaphore_wait(barrier, sides[0] * sides[1] * sides[2] - 1)
    first.send(pos, has)
    targets.send(pos, has)
    second.clear(has)

    u0, u1, u2 = (ulat.at[k] for k in range(3))
    firsts = [u0.at[c] for c in range(3)] + [wflat]
    goals = [iflat.at[c] for c in range(3)] + [pflat]

    def wide(group, targets, u):
        def inside(t, carry):
            stresses(grads, wflat, corners, 26 + 8 * t)
            return carry

        def outside(t, carry):
            stresses(grads, wflat, corners, jnp.where(t < 4, 0, 82) + 8 * t)
            return carry

        group.wait_recv(pos, has, False)
        group.to_flat(targets, False)
        for r in range(26, 130, 8):
            differences(u, grads, lane, r)
        lax.fori_loop(0, 11, inside, 0)
        group.wait_recv(pos, has, True)
        group.to_flat(targets, True)
        for r in (*range(0, 32, 8), *range(130, 162, 8)):
            differences(u, grads, lane, r)
        lax.fori_loop(0, 8, outside, 0)

    def narrow(u):
        for r in range(1, 11):
            differences(u, grads, lane, SLAB + r, SLAB)
        for r in (9 * SLAB + 1, 9 * SLAB + 3, 10 * SLAB + 1, 10 * SLAB + 3):
            differences(u, grads, lane, r)

        def column(t, carry):
            stresses(grads, wflat, corners, SLAB + 1 + t, SLAB)
            return carry

        lax.fori_loop(0, 10, column, 0)
        for r in (9 * SLAB + 1, 9 * SLAB + 3):
            stresses(grads, wflat, corners, r)

    def update_wide(u, prev, fresh, omega):
        for r in range(SLAB, SLAB + 136, 8):
            new = update({}, u, prev, iflat, rate, corners, omega, lane, r)
            for c in range(3):
                fresh[c, pl.ds(r, 8), :] = new[c]

    def update_own(u, prev, omega):
        state = {}
        return [
            update(state, u, prev, iflat, rate, corners, omega, lane, HALO * SLAB + r, SLAB)
            for r in range(HALO, HALO + BX + 1)
        ]

    def own_tile(rows, i, c):
        shift = 8 * (HALO + i) + HZ
        return pltpu.roll(jnp.where(lane >= shift, rows[i][c], rows[i + 1][c]), 128 - shift, 1)

    wide(first, firsts, u0)
    for edges in (False, True):
        targets.wait_recv(pos, has, edges)
        targets.to_flat(goals, edges)

    sums = grads.at[0]
    for r in range(SLAB, SLAB + 136, 8):
        sums[pl.ds(r, 8), :] = wflat[pl.ds(r, 8), :] + wflat[pl.ds(r - SLAB, 8), :]
    for r in range(SLAB, SLAB + 136, 8):

        def get(row):
            return sums[pl.ds(row, 8), :]

        total = (earlier(get, r, lane, EZ + 1) + earlier(get, r, lane, EZ)) + (
            earlier(get, r, lane, 1) + get(r)
        )
        rate[pl.ds(r, 8), :] = jnp.where(
            pflat[pl.ds(r, 8), :] > 0.0, 0.0, relax / (1.0 + 3.0 * total)
        )

    omega1 = 2.0 / (2.0 - radius * radius)
    omega2 = 4.0 / (4.0 - radius * radius * omega1)
    omega3 = 4.0 / (4.0 - radius * radius * omega2)

    update_wide(u0, None, u1, None)
    narrow(u1)
    rows = update_own(u1, u0, omega1)
    pack = [zero, zero]
    for i in range(BX):
        second.put(i, [own_tile(rows, i, c) for c in range(3)])
    for i in range(BX + 1):
        place = HALO + i
        for c in range(3):
            if i > 0:
                merge(pack, i % BX, c, 0, rows[i][c], lane4, 8 * place - HZ)
            if i < BX:
                merge(pack, i, c, 1, rows[i][c], lane4, 8 * place)
    second.seal(pack)
    second.send(pos, has)
    for i in range(BX + 1):
        for c in range(3):
            u2[c, pl.ds(HALO * SLAB + HALO + i, BX, stride=SLAB), :] = rows[i][c]

    wide(second, [u2.at[c] for c in range(3)], u2)
    update_wide(u2, u1, u0, omega2)
    narrow(u0)
    rows = update_own(u0, u2, omega3)
    for i in range(BX):
        for c in range(3):
            out[c, i] = 4.0 * own_tile(rows, i, c)
    first.wait_send(pos, has)
    targets.wait_send(pos, has)
    second.wait_send(pos, has)


def per_device(start_disp, inertial, material, pinned, stiffness):
    f = jnp.float32
    flat = (ROWS, 128)
    hbm = pl.BlockSpec(memory_space=pl.ANY)
    return pl.pallas_call(
        kernel,
        out_shape=jax.ShapeDtypeStruct(start_disp.shape, f),
        in_specs=[hbm, hbm, hbm, hbm, pl.BlockSpec(memory_space=pltpu.SMEM)],
        out_specs=pl.BlockSpec(memory_space=pltpu.VMEM),
        scratch_shapes=[
            pltpu.VMEM(start_disp.shape, f),
            pltpu.VMEM(inertial.shape, f),
            pltpu.VMEM(material.shape, jnp.int32),
            pltpu.VMEM(pinned.shape, jnp.int32),
            pltpu.SemaphoreType.DMA((4,)),
            pltpu.VMEM((3, 3, *flat), f),
            pltpu.VMEM(flat, f),
            pltpu.VMEM((3, *flat), f),
            pltpu.VMEM(flat, f),
            pltpu.VMEM(flat, f),
            pltpu.VMEM((9, *flat), f),
            pltpu.VMEM((12, *flat), f),
            *Group.scratch(HALO, True, 4),
            *Group.scratch(1, True, 4),
            *Group.scratch(HALO, False, 3),
        ],
        compiler_params=pltpu.CompilerParams(
            collective_id=0, has_side_effects=True, vmem_limit_bytes=16 * 1024 * 1024
        ),
    )(start_disp, inertial, material, pinned, stiffness)


def solution(mesh):
    placed = (
        P(None, "gx", "gy", "gz"),
        P(None, "gx", "gy", "gz"),
        P("gx", "gy", "gz"),
        P("gx", "gy", "gz"),
        P(),
    )
    return jax.shard_map(
        per_device, mesh=mesh, in_specs=placed, out_specs=P(None, "gx", "gy", "gz"), check_vma=False
    )
```

time: 30.5 us -> 31 us (1.016)
  the two profiles are of different devices: /device:TPU:121 before, /device:TPU:6 now
where the time goes in v4:
time: 31 us; the launch traced here: 30.6 us
  Pallas kernels  26 us (84%)
  local copies, waits for them, and re-layouts  4.6 us (15%)
    pallas_call x1, Pallas kernels, per_device(): pl.pallas_call(kernel, out_shape=jax.ShapeDtypeStruct(start_disp.shape, f...  26 us
    unnamed x11, local copies, waits for them, and re-layouts  4.6 us

profile of v4, /device:TPU:6, one launch (start us, length us, event | category | flops | bytes accessed | tf_op | source)
XLA Modules:
  0.0 30.6 jit_solution(8462175616564223015)
XLA Ops:
  0.0 0.0 copy-start
  0.0 0.9 %copy-done = f32[3,8,8,128]{3,2,1,0:T(8,128)S(1)} copy-done((f32[3,8,8,128]{3,2,1,0:T(8,128)S(1)}, f32[3,8,8,128]{3,2,1,0:T(8,128)}, u32[]{:S(2)}) %copy-start) | copy-done | bytes 98328
  0.9 0.0 copy-start.1
  0.9 0.9 %copy-done.1 = f32[3,8,8,128]{3,2,1,0:T(8,128)S(1)} copy-done((f32[3,8,8,128]{3,2,1,0:T(8,128)S(1)}, f32[3,8,8,128]{3,2,1,0:T(8,128)}, u32[]{:S(2)}) %copy-start.1) | copy-done | bytes 98328
  1.8 0.0 copy-start.2
  1.8 0.8 %copy-done.2 = s32[8,8,128]{2,1,0:T(8,128)S(1)} copy-done((s32[8,8,128]{2,1,0:T(8,128)S(1)}, s32[8,8,128]{2,1,0:T(8,128)}, u32[]{:S(2)}) %copy-start.2) | copy-done | bytes 32792
  2.5 0.0 copy-start.3
  2.5 0.8 %copy-done.3 = s32[8,8,128]{2,1,0:T(8,128)S(1)} copy-done((s32[8,8,128]{2,1,0:T(8,128)S(1)}, s32[8,8,128]{2,1,0:T(8,128)}, u32[]{:S(2)}) %copy-start.3) | copy-done | bytes 32792
  3.3 0.0 copy-start.4
  3.3 0.7 %copy-done.4 = f32[8]{0:T(128)S(1)} copy-done((f32[8]{0:T(128)S(1)}, f32[8]{0:T(128)}, u32[]{:S(2)}) %copy-start.4) | copy-done | bytes 56
  4.0 26.0 %shard_map.55 = f32[3,8,8,128]{3,2,1,0:T(8,128)S(1)} custom-call(f32[3,8,8,128]{3,2,1,0:T(8,128)S(1)} %copy-done, f32[3,8,8,128]{3,2,1,0:T(8,128)S(1)} %copy-done.1, s32[8,8,128]{2,1,0:T(8,128)S(1)} %copy-done.2, s32[8,8,128]{2,1,0:T(8,128)S(1)} %copy-done.3, f32[8]{0:T(128)S(1)} %copy-done.4), custom_call_target="tpu_custom_call" | custom-call | tf_op jit(solution)/shard_map/pallas_call | solution.py:565
  29.9 0.6 %copy.7 = f32[3,8,8,128]{3,2,1,0:T(8,128)} copy(f32[3,8,8,128]{3,2,1,0:T(8,128)S(1)} %shard_map.55) | data formatting | bytes 196608
Async XLA Ops:
  0.0 0.9 %copy-start = (f32[3,8,8,128]{3,2,1,0:T(8,128)S(1)}, f32[3,8,8,128]{3,2,1,0:T(8,128)}, u32[]{:S(2)}) copy-start(f32[3,8,8,128]{3,2,1,0:T(8,128)} %start_hbm.1) | copy-start | bytes 294916
  0.9 0.9 %copy-start.1 = (f32[3,8,8,128]{3,2,1,0:T(8,128)S(1)}, f32[3,8,8,128]{3,2,1,0:T(8,128)}, u32[]{:S(2)}) copy-start(f32[3,8,8,128]{3,2,1,0:T(8,128)} %inertial_hbm.1) | copy-start | bytes 294916
  1.8 0.8 %copy-start.2 = (s32[8,8,128]{2,1,0:T(8,128)S(1)}, s32[8,8,128]{2,1,0:T(8,128)}, u32[]{:S(2)}) copy-start(s32[8,8,128]{2,1,0:T(8,128)} %material_hbm.1) | copy-start | bytes 98308
  2.5 0.8 %copy-start.3 = (s32[8,8,128]{2,1,0:T(8,128)S(1)}, s32[8,8,128]{2,1,0:T(8,128)}, u32[]{:S(2)}) copy-start(s32[8,8,128]{2,1,0:T(8,128)} %pinned_hbm.1) | copy-start | bytes 98308
  3.3 0.7 %copy-start.4 = (f32[8]{0:T(128)S(1)}, f32[8]{0:T(128)}, u32[]{:S(2)}) copy-start(f32[8]{0:T(128)} %stiffness.1) | copy-start | bytes 100

commit v5 on v4

--- a/solution.py
+++ b/solution.py
@@ -584,9 +584,7 @@
             *Group.scratch(1, True, 4),
             *Group.scratch(HALO, False, 3),
         ],
-        compiler_params=pltpu.CompilerParams(
-            collective_id=0, has_side_effects=True, vmem_limit_bytes=16 * 1024 * 1024
-        ),
+        compiler_params=pltpu.CompilerParams(collective_id=0, has_side_effects=True),
     )(start_disp, inertial, material, pinned, stiffness)
 
 

time: 31 us -> 28.2 us (0.910)
  local copies, waits for them, and re-layouts: 4.6 us -> 1.54 us
  Pallas kernels: 26 us -> 26.4 us
    unnamed x11 -> x1, local copies, waits for them, and re-layouts: 4.6 us -> 1.54 us
    pallas_call x1, Pallas kernels: 26 us -> 26.4 us  [per_device(): pl.pallas_call(kernel, out_shape=jax.ShapeDtypeStruct(start_disp.shape, f...]
where the time goes in v5:
time: 28.2 us; the launch traced here: 27.9 us
  Pallas kernels  26.4 us (94%)
  local copies, waits for them, and re-layouts  1.54 us (5%)
    pallas_call x1, Pallas kernels, per_device(): pl.pallas_call(kernel, out_shape=jax.ShapeDtypeStruct(start_disp.shape, f...  26.4 us
    unnamed x1, local copies, waits for them, and re-layouts  1.54 us

profile of v5, /device:TPU:6, one launch (start us, length us, event | category | flops | bytes accessed | tf_op | source)
XLA Modules:
  0.0 27.9 jit_solution(15531441923628442098)
XLA Ops:
  0.0 26.4 %shard_map.55 = f32[3,8,8,128]{3,2,1,0:T(8,128)} custom-call(f32[3,8,8,128]{3,2,1,0:T(8,128)} %start_hbm.1, f32[3,8,8,128]{3,2,1,0:T(8,128)} %inertial_hbm.1, s32[8,8,128]{2,1,0:T(8,128)} %material_hbm.1, s32[8,8,128]{2,1,0:T(8,128)} %pinned_hbm.1, f32[8]{0:T(128)} %stiffness.1), custom_call_target="tpu_custom_call" | custom-call | tf_op jit(solution)/shard_map/pallas_call | solution.py:565
  26.4 1.5 %copy.7 = f32[3,8,8,128]{3,2,1,0:T(8,128)} copy(f32[3,8,8,128]{3,2,1,0:T(8,128)} %shard_map.55) | data formatting | bytes 196608

commit v6 on v5

--- a/solution.py
+++ b/solution.py
@@ -23,7 +23,7 @@
 SLAB = 13
 ROWS = 176
 VOFF = 16
-ROLLED = 20
+TOGETHER = 2
 DIRS = [
     (dx, dy, dz)
     for dx in (-1, 0, 1)
@@ -240,22 +240,15 @@
         merge(packs, i, c, 1, tile, lane4, 128 - HZ)
 
 
-def loop(start, rows, step, body, unroll=1):
-    blocks = -(-rows // step)
-    unroll = min(unroll, blocks)
-
+def loop(count, body):
     def trip(t, carry):
-        for k in range(unroll):
-            body(start + t * (unroll * step) + k * step)
+        for k in range(TOGETHER):
+            body(t * TOGETHER + k)
         return carry
 
-    trips = blocks // unroll
-    if trips > 1:
-        lax.fori_loop(0, trips, trip, 0)
-    else:
-        trip(0, 0)
-    for k in range(trips * unroll, blocks):
-        body(start + k * step)
+    lax.fori_loop(0, count // TOGETHER, trip, 0)
+    for k in range(count - count % TOGETHER, count):
+        body(k)
 
 
 def span(row, stride):
@@ -299,35 +292,55 @@
         deform.append([fx, fy, fz])
     for c in range(3):
         deform[c][c] = deform[c][c] + 1.0
-    rows_sq = [
-        deform[c][0] * deform[c][0] + deform[c][1] * deform[c][1] + deform[c][2] * deform[c][2]
-        for c in range(3)
-    ]
-    total = rows_sq[0] + rows_sq[1] + rows_sq[2]
-    scale = jnp.minimum(lax.rsqrt(total * (2.0 / 3.0)), 0.5**0.5)
-    y = [[deform[c][d] * scale for d in range(3)] for c in range(3)]
+    def dot(i, j):
+        return deform[0][i] * deform[0][j] + deform[1][i] * deform[1][j] + deform[2][i] * deform[2][j]
+
+    grams = [dot(0, 0), dot(1, 1), dot(2, 2)]
+    total = grams[0] + grams[1] + grams[2]
+    scale = jnp.minimum(lax.rsqrt(total * (1.0 / 3.0)), 1.0)
+    half = scale * scale * 0.5
+    mean = half * total * (1.0 / 3.0)
+    d0, d1, d2 = (grams[k] * half - mean for k in range(3))
+    d01, d02, d12 = dot(0, 1) * half, dot(0, 2) * half, dot(1, 2) * half
+    sq01, sq02, sq12 = d01 * d01, d02 * d02, d12 * d12
+    e0, e1, e2 = d0 * d0 + (sq01 + sq02), d1 * d1 + (sq01 + sq12), d2 * d2 + (sq02 + sq12)
+    e01, e02, e12 = d02 * d12 - d2 * d01, d01 * d12 - d1 * d02, d01 * d02 - d0 * d12
+    p = 0.5 * (e0 + e1 + e2)
+    q = d0 * (d1 * d2 - sq12) + (d01 * e01 + d02 * e02)
+
+    def reduced(c0, c1, c2, c3, c4):
+        return c0 + q * c3, c1 + (p * c3 + q * c4), c2 + p * c4
+
+    def times_linear(k, c):
+        return k * c[0] + q * c[2], (k * c[1] + c[0]) + p * c[2], k * c[2] + c[1]
+
+    low = mean - 1.5
+    square = low * low
+    t = mean * square + q, 2.0 * (mean * low) + (square + p), mean + 2.0 * low
+    poly = times_linear(low, (t[0] - 1.5, t[1], t[2]))
+    for step in range(2, POLAR_STEPS):
+        c0, c1, c2 = poly
+        twice0, twice1 = c0 + c0, c1 + c1
+        square = reduced(c0 * c0, twice0 * c1, twice0 * c2 + c1 * c1, twice1 * c2, c2 * c2)
+        t0, t1, t2 = times_linear(mean, square)
+        t0 = t0 - 1.5
+        poly = reduced(
+            c0 * t0,
+            c0 * t1 + c1 * t0,
+            c0 * t2 + c1 * t1 + c2 * t0,
+            c1 * t2 + c2 * t1,
+            c2 * t2,
+        )
     weight = weights[span(row, stride), :]
-    heavy = weight * 2.0**0.5
-    for step in range(POLAR_STEPS):
-
-        def gram(i, j):
-            return y[0][i] * y[0][j] + y[1][i] * y[1][j] + y[2][i] * y[2][j]
-
-        d0, d1, d2 = 1.5 - gram(0, 0), 1.5 - gram(1, 1), 1.5 - gram(2, 2)
-        o01, o02, o12 = gram(0, 1), gram(0, 2), gram(1, 2)
-        if step == POLAR_STEPS - 1:
-            d0, d1, d2 = d0 * heavy, d1 * heavy, d2 * heavy
-            o01, o02, o12 = o01 * heavy, o02 * heavy, o12 * heavy
-        y = [
-            [
-                y[c][0] * d0 - (y[c][1] * o01 + y[c][2] * o02),
-                y[c][1] * d1 - (y[c][0] * o01 + y[c][2] * o12),
-                y[c][2] * d2 - (y[c][0] * o02 + y[c][1] * o12),
-            ]
-            for c in range(3)
-        ]
+    heavy = weight * scale
+    c0, c1, c2 = weight - heavy * poly[0], heavy * poly[1], heavy * poly[2]
+    w0, w1, w2 = (c0 - (c1 * d + c2 * e) for d, e in ((d0, e0), (d1, e1), (d2, e2)))
+    w01, w02, w12 = (c1 * d + c2 * e for d, e in ((d01, e01), (d02, e02), (d12, e12)))
     for c in range(3):
-        px, py, pz = (weight * deform[c][d] - y[c][d] for d in range(3))
+        fx, fy, fz = deform[c]
+        px = fx * w0 - (fy * w01 + fz * w02)
+        py = fy * w1 - (fx * w01 + fz * w12)
+        pz = fz * w2 - (fx * w02 + fy * w12)
         s, t = py + px, py - px
         for k, part in enumerate((s + pz, s - pz, t + pz, t - pz)):
             corners[4 * c + k, span(row + VOFF, stride), :] = part
@@ -453,24 +466,22 @@
     goals = [iflat.at[c] for c in range(3)] + [pflat]
 
     def wide(group, targets, u):
-        def inside(t, carry):
+        def inside(t):
             stresses(grads, wflat, corners, 26 + 8 * t)
-            return carry
-
-        def outside(t, carry):
+
+        def outside(t):
             stresses(grads, wflat, corners, jnp.where(t < 4, 0, 82) + 8 * t)
-            return carry
 
         group.wait_recv(pos, has, False)
         group.to_flat(targets, False)
         for r in range(26, 130, 8):
             differences(u, grads, lane, r)
-        lax.fori_loop(0, 11, inside, 0)
+        loop(12, inside)
         group.wait_recv(pos, has, True)
         group.to_flat(targets, True)
         for r in (*range(0, 32, 8), *range(130, 162, 8)):
             differences(u, grads, lane, r)
-        lax.fori_loop(0, 8, outside, 0)
+        loop(8, outside)
 
     def narrow(u):
         for r in range(1, 11):
@@ -478,11 +489,10 @@
         for r in (9 * SLAB + 1, 9 * SLAB + 3, 10 * SLAB + 1, 10 * SLAB + 3):
             differences(u, grads, lane, r)
 
-        def column(t, carry):
+        def column(t):
             stresses(grads, wflat, corners, SLAB + 1 + t, SLAB)
-            return carry
-
-        lax.fori_loop(0, 10, column, 0)
+
+        loop(10, column)
         for r in (9 * SLAB + 1, 9 * SLAB + 3):
             stresses(grads, wflat, corners, r)
 

time: 28.2 us -> 26.8 us (0.950)
  Pallas kernels: 26.4 us -> 24.9 us
    pallas_call x1, Pallas kernels: 26.4 us -> 24.9 us  [per_device(): pl.pallas_call(kernel, out_shape=jax.ShapeDtypeStruct(start_disp.shape, f...]
where the time goes in v6:
time: 26.8 us; the launch traced here: 26.5 us
  Pallas kernels  24.9 us (93%)
  local copies, waits for them, and re-layouts  1.54 us (6%)
    pallas_call x1, Pallas kernels, per_device(): pl.pallas_call(kernel, out_shape=jax.ShapeDtypeStruct(start_disp.shape, f...  24.9 us
    unnamed x1, local copies, waits for them, and re-layouts  1.54 us

profile of v6, /device:TPU:6, one launch (start us, length us, event | category | flops | bytes accessed | tf_op | source)
XLA Modules:
  0.0 26.5 jit_solution(14978234255010936779)
XLA Ops:
  0.0 24.9 %shard_map.55 = f32[3,8,8,128]{3,2,1,0:T(8,128)} custom-call(f32[3,8,8,128]{3,2,1,0:T(8,128)} %start_hbm.1, f32[3,8,8,128]{3,2,1,0:T(8,128)} %inertial_hbm.1, s32[8,8,128]{2,1,0:T(8,128)} %material_hbm.1, s32[8,8,128]{2,1,0:T(8,128)} %pinned_hbm.1, f32[8]{0:T(128)} %stiffness.1), custom_call_target="tpu_custom_call" | custom-call | tf_op jit(solution)/shard_map/pallas_call | solution.py:575
  24.9 1.5 %copy.7 = f32[3,8,8,128]{3,2,1,0:T(8,128)} copy(f32[3,8,8,128]{3,2,1,0:T(8,128)} %shard_map.55) | data formatting | bytes 196608

commit v7 on v6

--- a/solution.py
+++ b/solution.py
@@ -45,120 +45,85 @@
         pl.when(cond)(act)
 
 
+def zero(ref, index):
+    ref[index] = jnp.zeros(ref.at[index].shape, jnp.float32)
+
+
 class Group:
-    def __init__(self, width, dz, refs):
+    fields = 4
+
+    def __init__(self, width, refs):
         self.h = width
-        self.dz = dz
-        self.ro, self.ry, self.sy, self.szo, self.szy, self.zo, self.zy, self.ssem, self.rsem = refs
-        self.count = self.ro.shape[0]
-        if dz:
-            self.messages = list(DIRS)
-        else:
-            flat = [d for d in DIRS if d[2] == 0]
-            self.messages = flat + [(*d[:2], None) for d in flat]
+        self.ro, self.ry, self.sy, self.ssem, self.rsem, *self.extra = refs
+        self.messages = [d for d in DIRS if d[2] == 0]
 
     @staticmethod
-    def scratch(width, dz, count):
+    def scratch(width, total, extra=()):
         f = jnp.float32
-        sides = 2 if dz else 1
-        total = len(DIRS) if dz else 16
         return [
-            pltpu.VMEM((count, EX, BX, 128), f),
-            pltpu.VMEM((count, EX, 2, width, 128), f),
-            pltpu.VMEM((count, BX, 2, width, 128), f),
-            pltpu.VMEM((2, BX, 128), f),
-            pltpu.VMEM((2, 2, width, 128), f),
-            pltpu.VMEM((sides, 3, 2, BX, 128), f),
-            pltpu.VMEM((sides, 3, 2, 2, width, 128), f),
+            pltpu.VMEM((4, EX, BX, 128), f),
+            pltpu.VMEM((4, EX, 2, width, 128), f),
+            pltpu.VMEM((4, BX, 2, width, 128), f),
             pltpu.SemaphoreType.DMA((total,)),
             pltpu.SemaphoreType.DMA((total,)),
+            *(pltpu.VMEM(shape, f) for shape in extra),
         ]
 
-    def copy(self, index, pos):
-        dx, dy, dz = self.messages[index]
+    def parts(self, d):
+        dx, dy, _ = d
         h = self.h
         src_x = {-1: (0, h), 0: (0, BX), 1: (BX - h, h)}[dx]
         dst_x = {-1: (HALO + BX, h), 0: (HALO, BX), 1: (HALO - h, h)}[dx]
-        src_side, dst_side = {-1: (0, 1), 0: (0, 0), 1: (1, 0)}[dy]
-        zside = 1 if dz == -1 else 0
-        slot = 1 - dx
-        sx, tx = pl.ds(*src_x), pl.ds(*dst_x)
-        if dz == 0:
-            if dy == 0:
-                src = self.ro.at[:, pl.ds(HALO + src_x[0], src_x[1])]
-                dst = self.ro.at[:, tx]
-            else:
-                src, dst = self.sy.at[:, sx, src_side], self.ry.at[:, tx, dst_side]
-        elif dy == 0:
-            src, dst = self.szo, self.zo.at[zside, slot]
-        else:
-            src, dst = self.szy.at[:, src_side], self.zy.at[zside, slot, :, dst_side]
+        count = self.fields if dx == 0 else 4
+        fields, sx, tx = pl.ds(0, count), pl.ds(*src_x), pl.ds(*dst_x)
+        if dy == 0:
+            return self.ro.at[:, pl.ds(HALO + src_x[0], src_x[1])], self.ro.at[:, tx]
+        src_side, dst_side = (0, 1) if dy == -1 else (1, 0)
+        return self.sy.at[fields, sx, src_side], self.ry.at[fields, tx, dst_side]
+
+    def copy(self, index, pos):
+        d = self.messages[index]
+        src, dst = self.parts(d)
         return pltpu.make_async_remote_copy(
             src_ref=src,
             dst_ref=dst,
             send_sem=self.ssem.at[index],
             recv_sem=self.rsem.at[index],
-            device_id={a: p + d for a, p, d in zip(AXES, pos, (dx, dy, dz or 0))},
+            device_id={a: p + (e or 0) for a, p, e in zip(AXES, pos, d)},
             device_id_type=pl.DeviceIdType.MESH,
         )
 
-    def put(self, i, tiles):
+    def put(self, i, tiles, field=0):
         h = self.h
         for c, tile in enumerate(tiles):
-            self.ro[c, HALO + i] = tile
-            self.sy[c, i, 0] = tile[0:h]
-            self.sy[c, i, 1] = tile[BX - h : BX]
-
-    def seal(self, packs):
-        h = self.h
-        for k, pack in enumerate(packs):
-            self.szo[k] = pack
-            self.szy[k, 0] = pack[0:h]
-            self.szy[k, 1] = pack[BX - h : BX]
+            self.ro[field + c, HALO + i] = tile
+            self.sy[field + c, i, 0] = tile[0:h]
+            self.sy[field + c, i, 1] = tile[BX - h : BX]
 
     def clear(self, has):
-        h = self.h
-        zsides = self.zo.shape[0]
-
-        def zero(ref, index):
-            ref[index] = jnp.zeros(ref.at[index].shape, jnp.float32)
-
         for d in (-1, 1):
-            start = HALO + BX if d == 1 else HALO - h
+            start = HALO + BX if d == 1 else HALO - self.h
             side = 0 if d == -1 else 1
-            slot = 1 + d
-
-            def clear_x(start=start, slot=slot):
-                for c in range(self.count):
-                    for x in range(start, start + h):
+
+            def clear_x(start=start, slot=1 + d):
+                for c in range(4):
+                    for x in range(start, start + self.h):
                         zero(self.ro, (c, x))
                         zero(self.ry, (c, x))
-                for s in range(zsides):
-                    for k in range(2):
-                        zero(self.zo, (s, slot, k))
-                        zero(self.zy, (s, slot, k))
+                self.clear_columns(0, slot)
 
             pl.when(jnp.logical_not(has[0][d]))(clear_x)
 
             def clear_y(side=side):
-                for c in range(self.count):
+                for c in range(4):
                     for x in range(EX):
                         zero(self.ry, (c, x, side))
-                for s in range(zsides):
-                    for slot in range(3):
-                        for k in range(2):
-                            zero(self.zy, (s, slot, k, side))
+                self.clear_columns(1, side)
 
             pl.when(jnp.logical_not(has[1][d]))(clear_y)
 
-            def clear_z(side=side):
-                for slot in range(3):
-                    for k in range(2):
-                        zero(self.zo, (side, slot, k))
-                        zero(self.zy, (side, slot, k))
-
-            if self.dz:
-                pl.when(jnp.logical_not(has[2][d]))(clear_z)
+    def clear_columns(self, axis, which):
+        pass
 
     def send(self, pos, has):
         for index, d in sorted(enumerate(self.messages), key=lambda e: e[1][1] == 0):
@@ -174,15 +139,13 @@
         for index, d in enumerate(self.messages):
             guarded(every([has[a][d[a] or 0] for a in range(3)]), self.copy(index, pos).wait_send)
 
-    def to_flat(self, targets, edges):
+    def to_flat(self, targets, edges, kept=False):
         h = self.h
-        count = self.count
         rows = 2 * h if edges else BX
         lane = lax.broadcasted_iota(jnp.int32, (rows, 128), 1)
-        main, zs = (self.ry, self.zy) if edges else (self.ro, self.zo)
-        zero = jnp.zeros((rows, 128), jnp.float32)
-        kept = not (edges or self.dz)
-        before = [zero] * count
+        main = self.ry if edges else self.ro
+        nothing = jnp.zeros((rows, 128), jnp.float32)
+        before = [nothing] * len(targets)
         for place in range(SLAB):
             if kept and HALO < place < HALO + BX:
                 continue
@@ -192,17 +155,17 @@
 
             def columns(side, slot):
                 if kept and slot == 1:
-                    return zero
-                return zs[side, slot, unit // 4].reshape(rows, 128)
+                    return nothing
+                return self.columns(edges, side, slot, unit // 4)
 
             both = jnp.where(
                 (lane & 7) < HZ,
-                zero if first else columns(zs.shape[0] - 1, before_slot),
-                zero if last else columns(0, slot),
+                nothing if first else columns(1, before_slot),
+                nothing if last else columns(0, slot),
             )
-            for c in range(count):
+            for c, out in enumerate(targets):
                 if last or (kept and slot == 1):
-                    now = zero
+                    now = nothing
                 else:
                     now = pltpu.roll(main[c, place].reshape(rows, 128), 8 * place + HZ, 1)
                 ends = pltpu.roll(both, (8 * place - HZ - 32 * (unit % 4) - 8 * c) % 128, 1)
@@ -212,19 +175,116 @@
                     jnp.where(lane < 8 * place - HZ, before[c], ends),
                 )
                 before[c] = now
-                out = targets[c]
                 if not edges:
-                    span = pl.ds(HALO * SLAB + place, BX, stride=SLAB)
+                    where = pl.ds(HALO * SLAB + place, BX, stride=SLAB)
                     if kept and place == HALO:
-                        flat = jnp.where(lane < 8 * place, flat, out[span, :])
+                        flat = jnp.where(lane < 8 * place, flat, out[where, :])
                     if kept and place == HALO + BX:
-                        flat = jnp.where(lane < 8 * place, out[span, :], flat)
-                    out[span, :] = flat
+                        flat = jnp.where(lane < 8 * place, out[where, :], flat)
+                    out[where, :] = flat
                 elif h == 1:
                     out[pl.ds(SLAB + place, 2, stride=9 * SLAB), :] = flat
                 else:
                     out[pl.ds(place, 2, stride=SLAB), :] = flat[0:2]
                     out[pl.ds(10 * SLAB + place, 2, stride=SLAB), :] = flat[2:4]
+
+
+class First(Group):
+    extra_shapes = [
+        (4, BX, 128),
+        (4, 2, HALO, 128),
+        (2, 3, 4, BX, 128),
+        (2, 3, 4, 2, HALO, 128),
+    ]
+
+    def __init__(self, refs):
+        super().__init__(HALO, refs)
+        self.messages = list(DIRS)
+        self.szo, self.szy, self.zo, self.zy = self.extra
+
+    def parts(self, d):
+        dx, dy, dz = d
+        if dz == 0:
+            return super().parts(d)
+        side, slot = (0 if dz == 1 else 1), 1 - dx
+        if dy == 0:
+            return self.szo, self.zo.at[side, slot]
+        src_side, dst_side = (0, 1) if dy == -1 else (1, 0)
+        return self.szy.at[:, src_side], self.zy.at[side, slot, :, dst_side]
+
+    def seal(self, packs):
+        for k, pack in enumerate(packs):
+            self.szo[k] = pack
+            self.szy[k, 0] = pack[0:HALO]
+            self.szy[k, 1] = pack[BX - HALO : BX]
+
+    def clear(self, has):
+        super().clear(has)
+        for d in (-1, 1):
+
+            def clear_z(side=(0 if d == -1 else 1)):
+                self.clear_columns(2, side)
+
+            pl.when(jnp.logical_not(has[2][d]))(clear_z)
+
+    def clear_columns(self, axis, which):
+        for side in range(2):
+            for slot in range(3):
+                for k in range(4):
+                    if axis == 1:
+                        zero(self.zy, (side, slot, k, which))
+                    elif which == (slot if axis == 0 else side):
+                        zero(self.zo, (side, slot, k))
+                        zero(self.zy, (side, slot, k))
+
+    def columns(self, edges, side, slot, k):
+        if not edges:
+            return self.zo[side, slot, k]
+        return self.zy[side, slot, k].reshape(2 * HALO, 128)
+
+
+class Targets(Group):
+    def __init__(self, refs, first):
+        super().__init__(1, refs)
+        self.first = first
+
+    def columns(self, edges, side, slot, k):
+        found = self.first.columns(edges, side, slot, 2 + k)
+        return found[1:3] if edges else found
+
+
+class Second(Group):
+    fields = 3
+    extra_shapes = [(2, 2, HALO, 128), (2, 2, HALO, 128)]
+
+    def __init__(self, refs):
+        super().__init__(HALO, refs)
+        self.messages = self.messages + [(0, -1, None), (0, 1, None)]
+        self.szy, self.zy = self.extra
+
+    def parts(self, d):
+        if d[2] == 0:
+            return super().parts(d)
+        src_side, dst_side = (0, 1) if d[1] == -1 else (1, 0)
+        return self.szy.at[:, src_side], self.zy.at[:, dst_side]
+
+    def seal(self, packs):
+        for k, pack in enumerate(packs):
+            self.put(k, [pack], 3)
+            self.put(BX - HALO + k, [pack], 3)
+            self.szy[k, 0] = pack[0:HALO]
+            self.szy[k, 1] = pack[BX - HALO : BX]
+
+    def clear_columns(self, axis, which):
+        if axis == 1:
+            for k in range(2):
+                zero(self.zy, (k, which))
+
+    def columns(self, edges, side, slot, k):
+        if slot == 1:
+            return self.zy[k].reshape(2 * HALO, 128)
+        x = k if slot == 0 else HALO + BX + k
+        return self.ry[3, x].reshape(2 * HALO, 128) if edges else self.ro[3, x]
 
 
 def merge(packs, unit, field, half, tile, lane4, from_lane):
@@ -410,10 +470,10 @@
     ]
     for load in loads:
         load.start()
-    nine = len(group_refs) // 3
-    first = Group(HALO, True, group_refs[:nine])
-    targets = Group(1, True, group_refs[nine : 2 * nine])
-    second = Group(HALO, False, group_refs[2 * nine :])
+    ends = [5 + len(First.extra_shapes), 10 + len(First.extra_shapes)]
+    first = First(group_refs[: ends[0]])
+    targets = Targets(group_refs[ends[0] : ends[1]], first)
+    second = Second(group_refs[ends[1] :])
     barrier = pltpu.get_barrier_semaphore()
     for d in sorted(DIRS, key=lambda e: -sum(map(abs, e))):
 
@@ -437,14 +497,14 @@
     inner = (grid_y < BX * sizes[1] - 1) & (grid_z < 128 * sizes[2] - 1)
 
     lane4 = lane >> 2
-    zero = jnp.zeros((BX, 128), jnp.float32)
-    packs = [[zero, zero], [zero, zero]]
+    nothing = jnp.zeros((BX, 128), jnp.float32)
+    packs = [[nothing, nothing], [nothing, nothing]]
     for i in range(BX):
         pins = pinned_v[i] > 0
         goal = [inertial_v[c, i] * 0.25 for c in range(3)]
         disp = [jnp.where(pins, goal[c], start_v[c, i] * 0.25) for c in range(3)]
         kinds = material_v[i]
-        weight = zero
+        weight = nothing
         for m in range(MATS):
             weight = jnp.where(kinds == m, stiffness[m] * 0.0625, weight)
         valid = inner & (pos[0] * BX + i < BX * sizes[0] - 1)
@@ -452,8 +512,7 @@
         for group, pack, tiles in zip((first, targets), packs, fields):
             group.put(i, tiles)
             pack_block(pack, i, tiles, lane4)
-    first.seal(packs[0])
-    targets.seal(packs[1])
+    first.seal(packs[0] + packs[1])
 
     sides = [1 + (p > 0).astype(jnp.int32) + (p < n - 1).astype(jnp.int32) for p, n in zip(pos, sizes)]
     pl.semaphore_wait(barrier, sides[0] * sides[1] * sides[2] - 1)
@@ -465,7 +524,7 @@
     firsts = [u0.at[c] for c in range(3)] + [wflat]
     goals = [iflat.at[c] for c in range(3)] + [pflat]
 
-    def wide(group, targets, u):
+    def wide(group, fields, u, between):
         def inside(t):
             stresses(grads, wflat, corners, 26 + 8 * t)
 
@@ -473,12 +532,13 @@
             stresses(grads, wflat, corners, jnp.where(t < 4, 0, 82) + 8 * t)
 
         group.wait_recv(pos, has, False)
-        group.to_flat(targets, False)
+        group.to_flat(fields, False, group is second)
         for r in range(26, 130, 8):
             differences(u, grads, lane, r)
         loop(12, inside)
+        between()
         group.wait_recv(pos, has, True)
-        group.to_flat(targets, True)
+        group.to_flat(fields, True)
         for r in (*range(0, 32, 8), *range(130, 162, 8)):
             differences(u, grads, lane, r)
         loop(8, outside)
@@ -513,10 +573,13 @@
         shift = 8 * (HALO + i) + HZ
         return pltpu.roll(jnp.where(lane >= shift, rows[i][c], rows[i + 1][c]), 128 - shift, 1)
 
-    wide(first, firsts, u0)
-    for edges in (False, True):
-        targets.wait_recv(pos, has, edges)
-        targets.to_flat(goals, edges)
+    def goals_inside():
+        targets.wait_recv(pos, has, False)
+        targets.to_flat(goals, False)
+
+    wide(first, firsts, u0, goals_inside)
+    targets.wait_recv(pos, has, True)
+    targets.to_flat(goals, True)
 
     sums = grads.at[0]
     for r in range(SLAB, SLAB + 136, 8):
@@ -540,7 +603,7 @@
     update_wide(u0, None, u1, None)
     narrow(u1)
     rows = update_own(u1, u0, omega1)
-    pack = [zero, zero]
+    pack = [nothing, nothing]
     for i in range(BX):
         second.put(i, [own_tile(rows, i, c) for c in range(3)])
     for i in range(BX + 1):
@@ -556,16 +619,16 @@
         for c in range(3):
             u2[c, pl.ds(HALO * SLAB + HALO + i, BX, stride=SLAB), :] = rows[i][c]
 
-    wide(second, [u2.at[c] for c in range(3)], u2)
+    first.wait_send(pos, has)
+    targets.wait_send(pos, has)
+    wide(second, [u2.at[c] for c in range(3)], u2, lambda: None)
+    second.wait_send(pos, has)
     update_wide(u2, u1, u0, omega2)
     narrow(u0)
     rows = update_own(u0, u2, omega3)
     for i in range(BX):
         for c in range(3):
             out[c, i] = 4.0 * own_tile(rows, i, c)
-    first.wait_send(pos, has)
-    targets.wait_send(pos, has)
-    second.wait_send(pos, has)
 
 
 def per_device(start_disp, inertial, material, pinned, stiffness):
@@ -574,7 +637,7 @@
     hbm = pl.BlockSpec(memory_space=pl.ANY)
     return pl.pallas_call(
         kernel,
-        out_shape=jax.ShapeDtypeStruct(start_disp.shape, f),
+        out_shape=pltpu.VMEM(start_disp.shape, f),
         in_specs=[hbm, hbm, hbm, hbm, pl.BlockSpec(memory_space=pltpu.SMEM)],
         out_specs=pl.BlockSpec(memory_space=pltpu.VMEM),
         scratch_shapes=[
@@ -590,9 +653,9 @@
             pltpu.VMEM(flat, f),
             pltpu.VMEM((9, *flat), f),
             pltpu.VMEM((12, *flat), f),
-            *Group.scratch(HALO, True, 4),
-            *Group.scratch(1, True, 4),
-            *Group.scratch(HALO, False, 3),
+            *Group.scratch(HALO, len(DIRS), First.extra_shapes),
+            *Group.scratch(1, 8),
+            *Group.scratch(HALO, 10, Second.extra_shapes),
         ],
         compiler_params=pltpu.CompilerParams(collective_id=0, has_side_effects=True),
     )(start_disp, inertial, material, pinned, stiffness)

time: 26.8 us -> 24.9 us (0.929)
  local copies, waits for them, and re-layouts: 1.54 us -> 0.64 us
  Pallas kernels: 24.9 us -> 24 us
    pallas_call x1, Pallas kernels: 24.9 us -> 24 us  [per_device(): pl.pallas_call(kernel, out_shape=pltpu.VMEM(start_disp.shape, f), in_spec...]
    unnamed x1, local copies, waits for them, and re-layouts: 1.54 us -> 0.64 us
where the time goes in v7:
time: 24.9 us; the launch traced here: 24.7 us
  Pallas kernels  24 us (96%)
  local copies, waits for them, and re-layouts  0.64 us (3%)
    pallas_call x1, Pallas kernels, per_device(): pl.pallas_call(kernel, out_shape=pltpu.VMEM(start_disp.shape, f), in_spec...  24 us
    unnamed x1, local copies, waits for them, and re-layouts  0.64 us

profile of v7, /device:TPU:6, one launch (start us, length us, event | category | flops | bytes accessed | tf_op | source)
XLA Modules:
  0.0 24.7 jit_solution(3408782141637098147)
XLA Ops:
  0.0 24.0 %shard_map.55 = f32[3,8,8,128]{3,2,1,0:T(8,128)S(1)} custom-call(f32[3,8,8,128]{3,2,1,0:T(8,128)} %start_hbm.1, f32[3,8,8,128]{3,2,1,0:T(8,128)} %inertial_hbm.1, s32[8,8,128]{2,1,0:T(8,128)} %material_hbm.1, s32[8,8,128]{2,1,0:T(8,128)} %pinned_hbm.1, f32[8]{0:T(128)} %stiffness.1), custom_call_target="tpu_custom_call" | custom-call | tf_op jit(solution)/shard_map/pallas_call | solution.py:638
  24.0 0.6 %copy.7 = f32[3,8,8,128]{3,2,1,0:T(8,128)} copy(f32[3,8,8,128]{3,2,1,0:T(8,128)S(1)} %shard_map.55) | data formatting | bytes 196608

commit v8 on v7

--- a/solution.py
+++ b/solution.py
@@ -126,7 +126,9 @@
         pass
 
     def send(self, pos, has):
-        for index, d in sorted(enumerate(self.messages), key=lambda e: e[1][1] == 0):
+        for index, d in sorted(
+            enumerate(self.messages), key=lambda e: (e[1][1] == 0, -sum(abs(a or 0) for a in e[1]))
+        ):
             guarded(every([has[a][d[a] or 0] for a in range(3)]), self.copy(index, pos).start)
 
     def wait_recv(self, pos, has, edges):
@@ -531,11 +533,22 @@
         def outside(t):
             stresses(grads, wflat, corners, jnp.where(t < 4, 0, 82) + 8 * t)
 
-        group.wait_recv(pos, has, False)
-        group.to_flat(fields, False, group is second)
-        for r in range(26, 130, 8):
-            differences(u, grads, lane, r)
-        loop(12, inside)
+        def columns(numbers, shift):
+            for r in numbers:
+                differences(u, grads, lane, HALO * SLAB + r, SLAB)
+            loop(6, lambda t: stresses(grads, wflat, corners, HALO * SLAB + shift(t), SLAB))
+
+        if group is second:
+            columns(range(3, 9), lambda t: 3 + t)
+            group.wait_recv(pos, has, False)
+            group.to_flat(fields, False, True)
+            columns((0, 1, 2, 9, 10, 11), lambda t: t + jnp.where(t < 3, 0, 6))
+        else:
+            group.wait_recv(pos, has, False)
+            group.to_flat(fields, False)
+            for r in range(26, 130, 8):
+                differences(u, grads, lane, r)
+            loop(12, inside)
         between()
         group.wait_recv(pos, has, True)
         group.to_flat(fields, True)

time: 24.9 us -> 24.5 us (0.984)
  Pallas kernels: 24 us -> 23.7 us
    pallas_call x1, Pallas kernels: 24 us -> 23.7 us  [per_device(): pl.pallas_call(kernel, out_shape=pltpu.VMEM(start_disp.shape, f), in_spec...]
where the time goes in v8:
time: 24.5 us; the launch traced here: 24.4 us
  Pallas kernels  23.7 us (97%)
  local copies, waits for them, and re-layouts  0.64 us (3%)
    pallas_call x1, Pallas kernels, per_device(): pl.pallas_call(kernel, out_shape=pltpu.VMEM(start_disp.shape, f), in_spec...  23.7 us
    unnamed x1, local copies, waits for them, and re-layouts  0.64 us

profile of v8, /device:TPU:6, one launch (start us, length us, event | category | flops | bytes accessed | tf_op | source)
XLA Modules:
  0.0 24.4 jit_solution(5600022525332970051)
XLA Ops:
  0.0 23.7 %shard_map.55 = f32[3,8,8,128]{3,2,1,0:T(8,128)S(1)} custom-call(f32[3,8,8,128]{3,2,1,0:T(8,128)} %start_hbm.1, f32[3,8,8,128]{3,2,1,0:T(8,128)} %inertial_hbm.1, s32[8,8,128]{2,1,0:T(8,128)} %material_hbm.1, s32[8,8,128]{2,1,0:T(8,128)} %pinned_hbm.1, f32[8]{0:T(128)} %stiffness.1), custom_call_target="tpu_custom_call" | custom-call | tf_op jit(solution)/shard_map/pallas_call | solution.py:651
  23.7 0.6 %copy.7 = f32[3,8,8,128]{3,2,1,0:T(8,128)} copy(f32[3,8,8,128]{3,2,1,0:T(8,128)S(1)} %shard_map.55) | data formatting | bytes 196608

commit v9 on v8

--- a/solution.py
+++ b/solution.py
@@ -452,6 +452,7 @@
     iflat,
     pflat,
     rate,
+    sums,
     grads,
     corners,
     *group_refs,
@@ -569,11 +570,29 @@
         for r in (9 * SLAB + 1, 9 * SLAB + 3):
             stresses(grads, wflat, corners, r)
 
-    def update_wide(u, prev, fresh, omega):
-        for r in range(SLAB, SLAB + 136, 8):
+    inner = range(3 * SLAB, 9 * SLAB, 8)
+    outer = (*range(SLAB, 3 * SLAB, 8), *range(9 * SLAB, 11 * SLAB, 8))
+
+    def update_rows(blocks, u, prev, fresh, omega):
+        for r in blocks:
             new = update({}, u, prev, iflat, rate, corners, omega, lane, r)
             for c in range(3):
                 fresh[c, pl.ds(r, 8), :] = new[c]
+
+    def rates(blocks):
+        for r in blocks:
+            sums[pl.ds(r, 8), :] = wflat[pl.ds(r, 8), :] + wflat[pl.ds(r - SLAB, 8), :]
+
+        def get(row):
+            return sums[pl.ds(row, 8), :]
+
+        for r in blocks:
+            total = (earlier(get, r, lane, EZ + 1) + earlier(get, r, lane, EZ)) + (
+                earlier(get, r, lane, 1) + get(r)
+            )
+            rate[pl.ds(r, 8), :] = jnp.where(
+                pflat[pl.ds(r, 8), :] > 0.0, 0.0, relax / (1.0 + 3.0 * total)
+            )
 
     def update_own(u, prev, omega):
         state = {}
@@ -586,34 +605,21 @@
         shift = 8 * (HALO + i) + HZ
         return pltpu.roll(jnp.where(lane >= shift, rows[i][c], rows[i + 1][c]), 128 - shift, 1)
 
-    def goals_inside():
-        targets.wait_recv(pos, has, False)
-        targets.to_flat(goals, False)
-
-    wide(first, firsts, u0, goals_inside)
-    targets.wait_recv(pos, has, True)
-    targets.to_flat(goals, True)
-
-    sums = grads.at[0]
-    for r in range(SLAB, SLAB + 136, 8):
-        sums[pl.ds(r, 8), :] = wflat[pl.ds(r, 8), :] + wflat[pl.ds(r - SLAB, 8), :]
-    for r in range(SLAB, SLAB + 136, 8):
-
-        def get(row):
-            return sums[pl.ds(row, 8), :]
-
-        total = (earlier(get, r, lane, EZ + 1) + earlier(get, r, lane, EZ)) + (
-            earlier(get, r, lane, 1) + get(r)
-        )
-        rate[pl.ds(r, 8), :] = jnp.where(
-            pflat[pl.ds(r, 8), :] > 0.0, 0.0, relax / (1.0 + 3.0 * total)
-        )
-
     omega1 = 2.0 / (2.0 - radius * radius)
     omega2 = 4.0 / (4.0 - radius * radius * omega1)
     omega3 = 4.0 / (4.0 - radius * radius * omega2)
 
-    update_wide(u0, None, u1, None)
+    def inner_first():
+        targets.wait_recv(pos, has, False)
+        targets.to_flat(goals, False)
+        rates(inner)
+        update_rows(inner, u0, None, u1, None)
+
+    wide(first, firsts, u0, inner_first)
+    targets.wait_recv(pos, has, True)
+    targets.to_flat(goals, True)
+    rates(outer)
+    update_rows(outer, u0, None, u1, None)
     narrow(u1)
     rows = update_own(u1, u0, omega1)
     pack = [nothing, nothing]
@@ -634,9 +640,14 @@
 
     first.wait_send(pos, has)
     targets.wait_send(pos, has)
-    wide(second, [u2.at[c] for c in range(3)], u2, lambda: None)
+    wide(
+        second,
+        [u2.at[c] for c in range(3)],
+        u2,
+        lambda: update_rows(inner, u2, u1, u0, omega2),
+    )
     second.wait_send(pos, has)
-    update_wide(u2, u1, u0, omega2)
+    update_rows(outer, u2, u1, u0, omega2)
     narrow(u0)
     rows = update_own(u0, u2, omega3)
     for i in range(BX):
@@ -664,6 +675,7 @@
             pltpu.VMEM((3, *flat), f),
             pltpu.VMEM(flat, f),
             pltpu.VMEM(flat, f),
+            pltpu.VMEM(flat, f),
             pltpu.VMEM((9, *flat), f),
             pltpu.VMEM((12, *flat), f),
             *Group.scratch(HALO, len(DIRS), First.extra_shapes),

time: 24.5 us -> 24.6 us (level)
  no operation moved by 1% of the time
where the time goes in v9:
time: 24.6 us; the launch traced here: 24.5 us
  Pallas kernels  23.8 us (97%)
  local copies, waits for them, and re-layouts  0.64 us (3%)
    pallas_call x1, Pallas kernels, per_device(): pl.pallas_call(kernel, out_shape=pltpu.VMEM(start_disp.shape, f), in_spec...  23.8 us
    unnamed x1, local copies, waits for them, and re-layouts  0.64 us

profile of v9, /device:TPU:6, one launch (start us, length us, event | category | flops | bytes accessed | tf_op | source)
XLA Modules:
  0.0 24.5 jit_solution(13011438494102892330)
XLA Ops:
  0.0 23.8 %shard_map.55 = f32[3,8,8,128]{3,2,1,0:T(8,128)S(1)} custom-call(f32[3,8,8,128]{3,2,1,0:T(8,128)} %start_hbm.1, f32[3,8,8,128]{3,2,1,0:T(8,128)} %inertial_hbm.1, s32[8,8,128]{2,1,0:T(8,128)} %material_hbm.1, s32[8,8,128]{2,1,0:T(8,128)} %pinned_hbm.1, f32[8]{0:T(128)} %stiffness.1), custom_call_target="tpu_custom_call" | custom-call | tf_op jit(solution)/shard_map/pallas_call | solution.py:662
  23.9 0.6 %copy.7 = f32[3,8,8,128]{3,2,1,0:T(8,128)} copy(f32[3,8,8,128]{3,2,1,0:T(8,128)S(1)} %shard_map.55) | data formatting | bytes 196608

commit v10 on v9

--- a/solution.py
+++ b/solution.py
@@ -127,7 +127,7 @@
 
     def send(self, pos, has):
         for index, d in sorted(
-            enumerate(self.messages), key=lambda e: (e[1][1] == 0, -sum(abs(a or 0) for a in e[1]))
+            enumerate(self.messages), key=lambda e: (e[1][1] != 0, -sum(abs(a or 0) for a in e[1]))
         ):
             guarded(every([has[a][d[a] or 0] for a in range(3)]), self.copy(index, pos).start)
 

time: 24.6 us -> 23.7 us (0.963)
  the two profiles are of different devices: /device:TPU:6 before, /device:TPU:89 now
where the time goes in v10:
time: 23.7 us; the launch traced here: 23.5 us
  Pallas kernels  22.9 us (97%)
  local copies, waits for them, and re-layouts  0.64 us (3%)
    pallas_call x1, Pallas kernels, per_device(): pl.pallas_call(kernel, out_shape=pltpu.VMEM(start_disp.shape, f), in_spec...  22.9 us
    unnamed x1, local copies, waits for them, and re-layouts  0.64 us

profile of v10, /device:TPU:89, one launch (start us, length us, event | category | flops | bytes accessed | tf_op | source)
XLA Modules:
  0.0 23.5 jit_solution(8109121441640549288)
XLA Ops:
  0.0 22.9 %shard_map.55 = f32[3,8,8,128]{3,2,1,0:T(8,128)S(1)} custom-call(f32[3,8,8,128]{3,2,1,0:T(8,128)} %start_hbm.1, f32[3,8,8,128]{3,2,1,0:T(8,128)} %inertial_hbm.1, s32[8,8,128]{2,1,0:T(8,128)} %material_hbm.1, s32[8,8,128]{2,1,0:T(8,128)} %pinned_hbm.1, f32[8]{0:T(128)} %stiffness.1), custom_call_target="tpu_custom_call" | custom-call | tf_op jit(solution)/shard_map/pallas_call | solution.py:662
  22.9 0.6 %copy.7 = f32[3,8,8,128]{3,2,1,0:T(8,128)} copy(f32[3,8,8,128]{3,2,1,0:T(8,128)S(1)} %shard_map.55) | data formatting | bytes 196608

commit v11 on v10

--- a/solution.py
+++ b/solution.py
@@ -209,10 +209,11 @@
         if dz == 0:
             return super().parts(d)
         side, slot = (0 if dz == 1 else 1), 1 - dx
+        tiles = pl.ds(0, 2 if dx == -1 else 4)
         if dy == 0:
-            return self.szo, self.zo.at[side, slot]
+            return self.szo.at[tiles], self.zo.at[side, slot, tiles]
         src_side, dst_side = (0, 1) if dy == -1 else (1, 0)
-        return self.szy.at[:, src_side], self.zy.at[side, slot, :, dst_side]
+        return self.szy.at[tiles, src_side], self.zy.at[side, slot, tiles, dst_side]
 
     def seal(self, packs):
         for k, pack in enumerate(packs):
@@ -239,10 +240,10 @@
                         zero(self.zo, (side, slot, k))
                         zero(self.zy, (side, slot, k))
 
-    def columns(self, edges, side, slot, k):
+    def columns(self, edges, side, slot, k, group=0):
         if not edges:
-            return self.zo[side, slot, k]
-        return self.zy[side, slot, k].reshape(2 * HALO, 128)
+            return self.zo[side, slot, 2 * k + group]
+        return self.zy[side, slot, 2 * k + group].reshape(2 * HALO, 128)
 
 
 class Targets(Group):
@@ -251,7 +252,7 @@
         self.first = first
 
     def columns(self, edges, side, slot, k):
-        found = self.first.columns(edges, side, slot, 2 + k)
+        found = self.first.columns(edges, side, slot, k, 1)
         return found[1:3] if edges else found
 
 
@@ -515,7 +516,7 @@
         for group, pack, tiles in zip((first, targets), packs, fields):
             group.put(i, tiles)
             pack_block(pack, i, tiles, lane4)
-    first.seal(packs[0] + packs[1])
+    first.seal([packs[g][k] for k in range(2) for g in range(2)])
 
     sides = [1 + (p > 0).astype(jnp.int32) + (p < n - 1).astype(jnp.int32) for p, n in zip(pos, sizes)]
     pl.semaphore_wait(barrier, sides[0] * sides[1] * sides[2] - 1)

time: 23.7 us -> 23.4 us (0.987)
  the two profiles are of different devices: /device:TPU:89 before, /device:TPU:2 now
where the time goes in v11:
time: 23.4 us; the launch traced here: 23.2 us
  Pallas kernels  22.6 us (97%)
  local copies, waits for them, and re-layouts  0.64 us (3%)
    pallas_call x1, Pallas kernels, per_device(): pl.pallas_call(kernel, out_shape=pltpu.VMEM(start_disp.shape, f), in_spec...  22.6 us
    unnamed x1, local copies, waits for them, and re-layouts  0.64 us

profile of v11, /device:TPU:2, one launch (start us, length us, event | category | flops | bytes accessed | tf_op | source)
XLA Modules:
  0.0 23.2 jit_solution(11908299442913646546)
XLA Ops:
  0.0 22.6 %shard_map.55 = f32[3,8,8,128]{3,2,1,0:T(8,128)S(1)} custom-call(f32[3,8,8,128]{3,2,1,0:T(8,128)} %start_hbm.1, f32[3,8,8,128]{3,2,1,0:T(8,128)} %inertial_hbm.1, s32[8,8,128]{2,1,0:T(8,128)} %material_hbm.1, s32[8,8,128]{2,1,0:T(8,128)} %pinned_hbm.1, f32[8]{0:T(128)} %stiffness.1), custom_call_target="tpu_custom_call" | custom-call | tf_op jit(solution)/shard_map/pallas_call | solution.py:663
  22.6 0.6 %copy.7 = f32[3,8,8,128]{3,2,1,0:T(8,128)} copy(f32[3,8,8,128]{3,2,1,0:T(8,128)S(1)} %shard_map.55) | data formatting | bytes 196608
